TPU v7x, 256 devices: a whole 4x4x8 slice. The times are simulated.
256 devices in a mesh: ta: 64 (over y, z_hi, x, core), ga: 4 (over z_lo).
Axes of the slice: x: 4, y: 4, z: 8 (z_hi: 2, z_lo: 4; z = z_hi * 4 + z_lo), core: 2. Of those that a mesh axis runs over, the one named last changes fastest.
Arguments:
- snapshots: bfloat16 [1024, 4, 131072], P('ta', 'ga'), may hold values from -12 to 12
- block_starts: int32 [7], replicated, may hold values from 0 to 768
- kept_freqs: int32 [32], replicated, may hold values from 0 to 128
Outputs:
- spectra: bfloat16 [4, 7, 2, 32, 131072], P('ga', None, None, None, 'ta')
- power_step: float32 [4, 7, 2, 32, 131072], P('ga', None, None, None, 'ta')
All inputs are finite; a program needn't handle non-finite values.
Results may differ from a plain program's by a relative error of at most 0.0047.
Values may be sent and summed in bfloat16 or wider, within the bound.
No kernel may reach another device: no remote copies, remote signals or barrier semaphores. Data moves between devices by JAX's collectives and lax.ppermute only.
A program may use at most 192 MiB of HBM per device.

v0:
```python
import functools
import math

import jax
import jax.numpy as jnp
from jax import lax
from jax.experimental import pallas as pl
from jax.experimental.pallas import tpu as pltpu
from jax.sharding import Mesh
from jax.sharding import PartitionSpec as P


NFFT = 256
NB = 7
NF = 32
HALF = NB * NF
ROWS = 2 * HALF
PAIRS = NB // 2
TA = ("y", "zh", "x", "c")
PLANE = ("y", "x", "c")
FIRST = 1024
WIDTH = 512
F32 = jnp.float32
BF16 = jnp.bfloat16
PARAMS = pltpu.CompilerParams(dimension_semantics=("arbitrary",), vmem_limit_bytes=60 * 2**20)


def weights(block_starts, kept_freqs, times):
    offset = times[None, :] - block_starts[:, None]
    inside = (offset >= 0) & (offset < NFFT)
    window = 0.5 - 0.5 * jnp.cos(2.0 * math.pi / NFFT * offset.astype(F32))
    scale = jnp.where(inside, window, 0.0)
    phase = kept_freqs[None, :, None] * jnp.where(inside, offset, 0)[:, None, :] % NFFT
    angle = 2.0 * math.pi / NFFT * phase.astype(F32)
    norm = 2.0 / math.sqrt(NFFT)
    real = scale[:, None, :] * jnp.cos(angle) * norm
    imag = -scale[:, None, :] * jnp.sin(angle) * norm
    table = jnp.stack([real, imag]).astype(BF16)
    return table.reshape(ROWS, times.shape[0])


def dot(a, b):
    return jnp.dot(a, b, preferred_element_type=F32)


def dot_t(a, b):
    return lax.dot_general(a, b, (((1,), (1,)), ((), ())), preferred_element_type=F32)


def same_freq(rows):
    row = lax.broadcasted_iota(jnp.int32, (rows, HALF), 0)
    col = lax.broadcasted_iota(jnp.int32, (rows, HALF), 1)
    return row % NF == col % NF


def pack_kernel(own, jobs, x_ref, *refs):
    outs, sems = refs[:-1], refs[-1]
    me = lax.axis_index("zh")
    copies = []
    for out, (shift, low) in zip(outs, jobs):
        side = (me + shift) % 2
        for d in range(out.shape[0]):
            start = ((d // 8) * 16 + d % 8) * own + low + side * (8 * own)
            cols = pl.ds(pl.multiple_of(start, 128), out.shape[2])
            copies.append(pltpu.make_async_copy(x_ref.at[:, cols], out.at[d], sems.at[len(copies)]))
    for copy in copies:
        copy.start()
    for copy in copies:
        copy.wait()


def pack(x, own, jobs):
    count = x.shape[1] // own // 2
    shapes = [jax.ShapeDtypeStruct((count, x.shape[0], n), x.dtype) for _, _, n in jobs]
    return pl.pallas_call(
        functools.partial(pack_kernel, own, [job[:2] for job in jobs]),
        out_shape=shapes,
        in_specs=[pl.BlockSpec(memory_space=pltpu.HBM)],
        out_specs=[pl.BlockSpec(memory_space=pltpu.VMEM)] * len(jobs),
        scratch_shapes=[pltpu.SemaphoreType.DMA((count * len(jobs),))],
        compiler_params=pltpu.CompilerParams(vmem_limit_bytes=60 * 2**20),
        name="pack",
    )(x)


def emit(parts, s_ref):
    for part in range(2):
        for b in range(NB):
            start = part * HALF + b * NF
            s_ref[b * 2 * NF + part * NF : b * 2 * NF + (part + 1) * NF, :] = parts[start : start + NF]


def gram_of(parts):
    real, imag = parts[:HALF], parts[HALF:]
    return dot_t(parts, real) + dot_t(jnp.concatenate([imag, -real], axis=0), imag)


def rows_of(ref):
    return ref[...].reshape(-1, ref.shape[2])


def whole_kernel(w0_ref, w1_ref, x0_ref, x1_ref, s_ref, g_ref):
    parts = (dot(w0_ref[...], rows_of(x0_ref)) + dot(w1_ref[...], rows_of(x1_ref))).astype(BF16)
    emit(parts, s_ref)
    gram = gram_of(parts)

    @pl.when(pl.program_id(0) == 0)
    def _():
        g_ref[...] = gram

    @pl.when(pl.program_id(0) > 0)
    def _():
        g_ref[...] += gram


def whole(w0, w1, x0, x1, pts):
    times = w0.shape[1]
    steps = x1.shape[2] // WIDTH
    fixed = pl.BlockSpec((ROWS, times), lambda i: (0, 0))
    moving = pl.BlockSpec((*x0.shape[:2], WIDTH), lambda i: (0, 0, i))
    return pl.pallas_call(
        whole_kernel,
        grid=(steps,),
        out_shape=(jax.ShapeDtypeStruct((ROWS, pts), BF16), jax.ShapeDtypeStruct((ROWS, HALF), F32)),
        in_specs=[fixed, fixed, moving, moving],
        out_specs=(pl.BlockSpec((ROWS, WIDTH), lambda i: (0, i)), pl.BlockSpec((ROWS, HALF), lambda i: (0, 0))),
        compiler_params=PARAMS,
        cost_estimate=pl.CostEstimate(flops=4 * ROWS * times * steps * WIDTH, bytes_accessed=2**22, transcendentals=0),
        name="whole",
    )(w0, w1, x0, x1)


def partial_kernel(w_ref, x_ref, p_ref):
    p_ref[...] = dot(w_ref[...], rows_of(x_ref))


def partial(w, x, first):
    times = w.shape[1]
    pts = x.shape[2] - first
    skip = first // WIDTH
    return pl.pallas_call(
        partial_kernel,
        grid=(pts // WIDTH,),
        out_shape=jax.ShapeDtypeStruct((ROWS, pts), F32),
        in_specs=[
            pl.BlockSpec((ROWS, times), lambda i: (0, 0)),
            pl.BlockSpec((*x.shape[:2], WIDTH), lambda i: (0, 0, i + skip)),
        ],
        out_specs=pl.BlockSpec((ROWS, WIDTH), lambda i: (0, i)),
        compiler_params=PARAMS,
        cost_estimate=pl.CostEstimate(flops=2 * ROWS * times * pts, bytes_accessed=2**21, transcendentals=0),
        name="partial",
    )(w, x)


def lane_block(rows):
    return lax.broadcasted_iota(jnp.int32, (rows, HALF), 1) // NF


def rest_kernel(steps, w_ref, x_ref, p_ref, g_ref, _, s_ref, t_ref, acc):
    step = pl.program_id(0)
    parts = (p_ref[...] + dot(w_ref[...], rows_of(x_ref))).astype(BF16)
    emit(parts, s_ref)
    gram = gram_of(parts)

    @pl.when(step == 0)
    def _():
        acc[...] = g_ref[...] + gram

    @pl.when(step > 0)
    def _():
        acc[...] += gram

    @pl.when(step == steps - 1)
    def _():
        kept = jnp.where(same_freq(ROWS), acc[...], 0.0)
        tables = kept.reshape(2 * NB, NF, HALF).sum(axis=1)
        block = lax.broadcasted_iota(jnp.int32, (NB, HALF), 0)
        t_ref[...] = jnp.zeros_like(t_ref)
        for k in range(PAIRS + 1):
            pick = (lane_block(NB) + k) % NB == block
            t_ref[k : k + 1, :HALF] = jnp.where(pick, tables[:NB], 0.0).sum(axis=0, keepdims=True)
            if k:
                row = PAIRS + k
                t_ref[row : row + 1, :HALF] = jnp.where(pick, tables[NB:], 0.0).sum(axis=0, keepdims=True)


def rest(w, x, p, g, s):
    times = w.shape[1]
    steps = x.shape[2] // WIDTH
    skip = s.shape[1] // WIDTH - steps
    return pl.pallas_call(
        functools.partial(rest_kernel, steps),
        grid=(steps,),
        out_shape=(jax.ShapeDtypeStruct(s.shape, BF16), jax.ShapeDtypeStruct((8, 256), F32)),
        in_specs=[
            pl.BlockSpec((ROWS, times), lambda i: (0, 0)),
            pl.BlockSpec((*x.shape[:2], WIDTH), lambda i: (0, 0, i)),
            pl.BlockSpec((ROWS, WIDTH), lambda i: (0, i)),
            pl.BlockSpec((ROWS, HALF), lambda i: (0, 0)),
            pl.BlockSpec(memory_space=pl.ANY),
        ],
        out_specs=(pl.BlockSpec((ROWS, WIDTH), lambda i: (0, i + skip)), pl.BlockSpec((8, 256), lambda i: (0, 0))),
        scratch_shapes=[pltpu.VMEM((ROWS, HALF), F32)],
        input_output_aliases={4: 0},
        compiler_params=PARAMS,
        cost_estimate=pl.CostEstimate(flops=2 * ROWS * times * steps * WIDTH, bytes_accessed=2**22, transcendentals=0),
        name="rest",
    )(w, x, p, g, s)


def turned(row, k):
    lane = lax.broadcasted_iota(jnp.int32, row.shape, 1)
    near = pltpu.roll(row, 256 - k * NF, 1)
    far = pltpu.roll(row, HALF - k * NF, 1)
    return jnp.where(lane < HALF - k * NF, near, far)


def power_kernel(denominator, t_ref, s_ref, o_ref, m_ref):
    @pl.when(pl.program_id(0) == 0)
    def _():
        sums = jnp.sum(t_ref[...], axis=0) / denominator
        real_rows = [sums[k : k + 1, :] for k in range(PAIRS + 1)]
        imag_rows = [jnp.zeros_like(real_rows[0])] + [sums[PAIRS + k : PAIRS + k + 1, :] for k in range(1, PAIRS + 1)]
        for k in range(PAIRS + 1, NB):
            real_rows.append(turned(real_rows[NB - k], k))
            imag_rows.append(-turned(imag_rows[NB - k], k))
        same = same_freq(NF)
        block = lane_block(1)
        for b in range(NB):
            re = sum(jnp.where((block + k) % NB == b, real_rows[k][:, :HALF], 0.0) for k in range(NB))
            im = sum(jnp.where((block + k) % NB == b, imag_rows[k][:, :HALF], 0.0) for k in range(NB))
            re = jnp.where(same, jnp.broadcast_to(re, (NF, HALF)), 0.0)
            im = jnp.where(same, jnp.broadcast_to(im, (NF, HALF)), 0.0)
            at = b * 2 * NF
            for part, (on_real, on_imag) in enumerate(((re, -im), (im, re))):
                for side, value in enumerate((on_real, on_imag)):
                    high = value.astype(BF16)
                    rows = slice(at + part * NF, at + (part + 1) * NF)
                    m_ref[2 * side, rows, :] = high
                    m_ref[2 * side + 1, rows, :] = (value - high.astype(F32)).astype(BF16)

    real = jnp.concatenate([s_ref[b * 2 * NF : b * 2 * NF + NF, :] for b in range(NB)], axis=0)
    imag = jnp.concatenate([s_ref[b * 2 * NF + NF : (b + 1) * 2 * NF, :] for b in range(NB)], axis=0)
    low = dot(m_ref[1], real) + dot(m_ref[3], imag)
    o_ref[...] = low + dot(m_ref[0], real) + dot(m_ref[2], imag)


def power(t, s, denominator):
    pts = s.shape[1]
    return pl.pallas_call(
        functools.partial(power_kernel, denominator),
        grid=(pts // WIDTH,),
        out_shape=jax.ShapeDtypeStruct((ROWS, pts), F32),
        in_specs=[
            pl.BlockSpec(t.shape, lambda i: (0, 0, 0)),
            pl.BlockSpec((ROWS, WIDTH), lambda i: (0, i)),
        ],
        out_specs=pl.BlockSpec((ROWS, WIDTH), lambda i: (0, i)),
        scratch_shapes=[pltpu.VMEM((4, ROWS, HALF), BF16)],
        compiler_params=PARAMS,
        name="power",
    )(t, s)


def to_all(t, axes):
    copies = jnp.broadcast_to(t[None], (lax.axis_size(axes), *t.shape))
    return lax.all_to_all(copies, axes, 0, 0, tiled=True)


def exchange(x, axes):
    return lax.all_to_all(x, axes, 0, 0, tiled=True)


def shards(snapshots, block_starts, kept_freqs):
    count = lax.axis_size(TA)
    local = snapshots.shape[0]
    own = snapshots.shape[2] // count
    total = own * count * lax.axis_size("zl")
    swap = [(0, 1), (1, 0)]
    x = snapshots.reshape(local, own * count)

    (first_out,) = pack(x, own, [(1, 0, FIRST)])
    first_in = lax.ppermute(first_out, "zh", swap)
    pass_on, mine = pack(x, own, [(1, FIRST, own - FIRST), (0, 0, own)])
    pass_on = exchange(pass_on, PLANE)
    side = lax.axis_index("zh")
    place = jnp.arange(local * count // 2, dtype=jnp.int32)
    times = place // 128 * 256 + place % 128
    w0 = weights(block_starts, kept_freqs, times + side * 128)
    w1 = weights(block_starts, kept_freqs, times + (1 - side) * 128)
    pass_on, w0, w1 = lax.optimization_barrier((pass_on, w0, w1))
    rest_in = lax.ppermute(pass_on, "zh", swap)
    x0 = exchange(mine, PLANE)
    x1 = exchange(first_in, PLANE)
    s, g = whole(w0, w1, x0, x1, own)
    p = partial(w0, x0, FIRST)
    s, t = rest(w1, rest_in, p, g, s)
    t = to_all(t, ("y", "x")).sum(axis=0)
    t = to_all(t, ("zh", "zl", "c"))
    out = power(t, s, float(NB * total))
    shape = (1, NB, 2, NF, own)
    return s.reshape(shape), out.reshape(shape)


def solution(mesh):
    split = Mesh(mesh.devices.reshape(4, 2, 4, 2, mesh.shape["ga"]), ("y", "zh", "x", "c", "zl"))
    out = P("zl", None, None, None, TA)
    return jax.shard_map(
        shards, mesh=split, in_specs=(P(TA, "zl", None), P(), P()), out_specs=(out, out), check_vma=False
    )
```

profile of v0, /device:TPU:1, one launch (start us, length us, event | category | flops | bytes accessed | tf_op | source)
XLA Modules:
  0.0 194.0 jit_solution(3739461933088567501)
XLA Ops:
  0.6 4.2 %pack.2 = (bf16[32,16,1024]{2,1,0:T(8,128)(2,1)}, bf16[32,16,2048]{2,1,0:T(8,128)(2,1)}) custom-call(bf16[16,131072]{1,0:T(8,128)(2,1)} %bitcast.5), custom_call_target="tpu_custom_call" | custom-call | tf_op jit(solution)/shard_map/pack/pallas_call | solution.py:75
  4.8 25.7 %all_to_all.25 = bf16[32,16,1024]{2,1,0:T(8,128)(2,1)} all-to-all(bf16[32,16,1024]{2,1,0:T(8,128)(2,1)} %get-tuple-element.11), channel_id=1, replica_groups=mesh['y'=4,'zh'=2,'x'=4,'c'=2,'zl'=4] {'y','x','c'}, dimensions={0} | all-to-all | bytes 2097152 | tf_op jit(solution)/shard_map/all_to_all | solution.py:272
  30.5 4.1 %all-to-all-start.1 = ((bf16[32,16,2048]{2,1,0:T(8,128)(2,1)}), bf16[32,16,2048]{2,1,0:T(8,128)(2,1)S(1)}, u32[]{:S(2)}, u32[]{:S(2)}) async-start(bf16[32,16,2048]{2,1,0:T(8,128)(2,1)} %get-tuple-element.15), calls=%async_computation.1 | async-start | bytes 4194304 | tf_op jit(solution)/shard_map/all_to_all | solution.py:272
  34.6 0.0 copy-start.3
  34.6 0.0 copy-start.4
  34.6 2.4 %pack.3 = bf16[32,16,1024]{2,1,0:T(8,128)(2,1)} custom-call(bf16[16,131072]{1,0:T(8,128)(2,1)} %bitcast.6), custom_call_target="tpu_custom_call" | custom-call | tf_op jit(solution)/shard_map/pack/pallas_call | solution.py:75
  37.1 7.0 %collective-permute-start.1 = (bf16[32,16,1024]{2,1,0:T(8,128)(2,1)}, bf16[32,16,1024]{2,1,0:T(8,128)(2,1)S(1)}, u32[]{:S(2)}, u32[]{:S(2)}) collective-permute-start(bf16[32,16,1024]{2,1,0:T(8,128)(2,1)} %pack.3), channel_id=1, source_target_pairs={{0,32},{32,0},{1,33},{33,1},{2,34},{34,2},{3,35},{35,3},{4,36},{36... | collective-permute-start | bytes 3145736 | tf_op jit(solution)/shard_map/ppermute | solution.py:284
  44.1 0.0 copy-done.3
  44.1 0.1 subtract_select_fusion
  44.2 0.2 fusion.15
  44.4 0.0 copy-done.4
  44.4 4.6 %multiply_convert_fusion.1 = (bf16[1,7,32,512]{3,2,1,0:T(8,128)(2,1)S(1)}, bf16[1,7,32,512]{3,2,1,0:T(8,128)(2,1)S(1)}, bf16[1,7,32,512]{3,2,1,0:T(8,128)(2,1)S(1)}, bf16[1,7,32,512]{3,2,1,0:T(8,128)(2,1)}) fusion(f32[7,512]{1,0:T(8,128)S(1)} %get-tuple-element.24, s32[7,512]{1,0:T(8,128)S(1)} %get-tuple-element.32, s32[32]{0:T(128)S(1)} %copy-done.4, ...), kind=kLoop, calls=%fused_computation.19 | loop fusion | flops 4587520 | bytes 1003648 | tf_op jit(solution)/shard_map/convert
  49.0 0.8 pad_maximum_fusion.1
  49.8 23.7 %collective-permute-done.1 = bf16[32,16,1024]{2,1,0:T(8,128)(2,1)S(1)} collective-permute-done((bf16[32,16,1024]{2,1,0:T(8,128)(2,1)}, bf16[32,16,1024]{2,1,0:T(8,128)(2,1)S(1)}, u32[]{:S(2)}, u32[]{:S(2)}) %collective-permute-start.1) | collective-permute-done | bytes 1048608 | tf_op jit(solution)/shard_map/ppermute | solution.py:284
  73.5 0.0 copy-start.2
  73.5 1.0 copy-done.2
  74.4 0.0 all-to-all-done.1.x_ref.x0_ref
  74.4 0.0 copy-start
  74.4 23.4 %all-to-all-start.2 = ((bf16[32,16,1024]{2,1,0:T(8,128)(2,1)}), bf16[32,16,1024]{2,1,0:T(8,128)(2,1)S(1)}, u32[]{:S(2)}, u32[]{:S(2)}) async-start(bf16[32,16,1024]{2,1,0:T(8,128)(2,1)} %copy-done.2), calls=%async_computation.2 | async-start | bytes 2097152 | tf_op jit(solution)/shard_map/all_to_all | solution.py:272
  97.8 1.8 pad_maximum_fusion
  99.6 6.0 %collective-permute-start = (bf16[32,16,1024]{2,1,0:T(8,128)(2,1)}, bf16[32,16,1024]{2,1,0:T(8,128)(2,1)}, u32[]{:S(2)}, u32[]{:S(2)}) collective-permute-start(bf16[32,16,1024]{2,1,0:T(8,128)(2,1)} %all_to_all.25), channel_id=1, source_target_pairs={{0,32},{32,0},{1,33},{33,1},{2,34},{34,2},{3,35},{35,3},{4,36},{36... | collective-permute-start | bytes 3145736 | tf_op jit(solution)/shard_map/ppermute | solution.py:293
  105.6 0.0 copy-done
  105.6 3.0 %partial.1.p_ref = f32[448,1024]{1,0:T(8,128)} custom-call(bf16[448,512]{1,0:T(8,128)(2,1)} %bitcast.8, bf16[32,16,2048]{2,1,0:T(8,128)(2,1)} %copy-done), custom_call_target="tpu_custom_call" | custom-call | flops 469762048 | bytes 2097152 | tf_op jit(solution)/shard_map/partial/pallas_call | solution.py:141
  108.6 6.7 %all-to-all-done.2.x1_ref = bf16[32,16,1024]{2,1,0:T(8,128)(2,1)S(1)} async-done(((bf16[32,16,1024]{2,1,0:T(8,128)(2,1)}), bf16[32,16,1024]{2,1,0:T(8,128)(2,1)S(1)}, u32[]{:S(2)}, u32[]{:S(2)}) %all-to-all-start.2) | async-done | bytes 1048608 | tf_op jit(solution)/shard_map/all_to_all | solution.py:272
  115.3 1.0 copy-done.1
  116.3 5.2 %whole.1 = (bf16[448,2048]{1,0:T(8,128)(2,1)}, f32[448,224]{1,0:T(8,128)}) custom-call(bf16[448,512]{1,0:T(8,128)(2,1)} %bitcast.9, bf16[448,512]{1,0:T(8,128)(2,1)} %bitcast.10, bf16[32,16,2048]{2,1,0:T(8,128)(2,1)} %copy-done, bf16[32,16,1024]{2,1,0:T(8,128)(2,1)} %copy-done.1), custom_call_target="tpu_custom_call" | custom-call | flops 939524096 | bytes 4194304 | tf_op jit(solution)/shard_map/whole/pallas_call | solution.py:121
  121.5 12.7 %collective-permute-done.x_ref = bf16[32,16,1024]{2,1,0:T(8,128)(2,1)} collective-permute-done((bf16[32,16,1024]{2,1,0:T(8,128)(2,1)}, bf16[32,16,1024]{2,1,0:T(8,128)(2,1)}, u32[]{:S(2)}, u32[]{:S(2)}) %collective-permute-start) | collective-permute-done | bytes 1048608 | tf_op jit(solution)/shard_map/ppermute | solution.py:293
  134.2 4.6 %rest.1 = (bf16[448,2048]{1,0:T(8,128)(2,1)}, f32[8,256]{1,0:T(8,128)}) custom-call(bf16[448,512]{1,0:T(8,128)(2,1)} %bitcast.11, bf16[32,16,1024]{2,1,0:T(8,128)(2,1)} %collective-permute-done.x_ref, f32[448,1024]{1,0:T(8,128)} %partial.1.p_ref, f32[448,224]{1,0:T(8,128)} %get-tuple-element.16.g_ref, ...), custom_call_target="tpu_custom_call", output_to_operand_aliasing={{0}: (4, {})} | custom-call | flops 469762048 | bytes 4194304 | tf_op jit(solution)/shard_map/rest/pallas_call | solution.py:192
  138.8 0.7 broadcast_in_dim.13
  139.5 13.2 %all_to_all.26 = f32[16,8,256]{2,1,0:T(8,128)S(1)} all-to-all(f32[16,8,256]{2,1,0:T(8,128)S(1)} %broadcast_in_dim.13), channel_id=1, replica_groups=mesh['y'=4,'zh'=2,'x'=4,'c'=2,'zl'=4] {'y','x'}, dimensions={0} | all-to-all | bytes 262144 | tf_op jit(solution)/shard_map/all_to_all | solution.py:268
  152.7 35.8 %all_to_all.27.t_ref = f32[16,8,256]{2,1,0:T(8,128)} all-to-all(f32[16,8,256]{2,1,0:T(8,128)S(1)} %broadcast_in_dim.14), channel_id=1, replica_groups=mesh['y'=4,'zh'=2,'x'=4,'c'=2,'zl'=4] {'zh','zl','c'}, dimensions={0} | all-to-all | bytes 262144 | tf_op jit(solution)/shard_map/all_to_all | solution.py:268
  188.5 5.5 %power.1 = f32[448,2048]{1,0:T(8,128)} custom-call(f32[16,8,256]{2,1,0:T(8,128)} %all_to_all.27.t_ref, bf16[448,2048]{1,0:T(8,128)(2,1)} %get-tuple-element.18.s_ref), custom_call_target="tpu_custom_call" | custom-call | tf_op jit(solution)/shard_map/power/pallas_call | solution.py:251
  (4 shorter events, 0.0 us)
Async XLA Ops:
  30.5 43.9 %all-to-all-start.1 = ((bf16[32,16,2048]{2,1,0:T(8,128)(2,1)}), bf16[32,16,2048]{2,1,0:T(8,128)(2,1)S(1)}, u32[]{:S(2)}, u32[]{:S(2)}) async-start(bf16[32,16,2048]{2,1,0:T(8,128)(2,1)} %get-tuple-element.15), calls=%async_computation.1 | async-start | bytes 4194304 | tf_op jit(solution)/shard_map/all_to_all | solution.py:272
  34.6 9.5 %copy-start.3 = (s32[7]{0:T(128)S(1)}, s32[7]{0:T(128)}, u32[]{:S(2)}) copy-start(s32[7]{0:T(128)} %param.4) | copy-start | bytes 88
  34.6 9.8 %copy-start.4 = (s32[32]{0:T(128)S(1)}, s32[32]{0:T(128)}, u32[]{:S(2)}) copy-start(s32[32]{0:T(128)} %param.5) | copy-start | bytes 388
  37.1 36.4 %collective-permute-start.1 = (bf16[32,16,1024]{2,1,0:T(8,128)(2,1)}, bf16[32,16,1024]{2,1,0:T(8,128)(2,1)S(1)}, u32[]{:S(2)}, u32[]{:S(2)}) collective-permute-start(bf16[32,16,1024]{2,1,0:T(8,128)(2,1)} %pack.3), channel_id=1, source_target_pairs={{0,32},{32,0},{1,33},{33,1},{2,34},{34,2},{3,35},{35,3},{4,36},{36... | collective-permute-start | bytes 3145736 | tf_op jit(solution)/shard_map/ppermute | solution.py:284
  73.5 1.0 copy-start.2
  74.4 31.2 %copy-start = (bf16[32,16,2048]{2,1,0:T(8,128)(2,1)}, bf16[32,16,2048]{2,1,0:T(8,128)(2,1)S(1)}, u32[]{:S(2)}) copy-start(bf16[32,16,2048]{2,1,0:T(8,128)(2,1)S(1)} %all-to-all-done.1.x_ref.x0_ref) | copy-start | bytes 6291460
  74.4 40.8 %all-to-all-start.2 = ((bf16[32,16,1024]{2,1,0:T(8,128)(2,1)}), bf16[32,16,1024]{2,1,0:T(8,128)(2,1)S(1)}, u32[]{:S(2)}, u32[]{:S(2)}) async-start(bf16[32,16,1024]{2,1,0:T(8,128)(2,1)} %copy-done.2), calls=%async_computation.2 | async-start | bytes 2097152 | tf_op jit(solution)/shard_map/all_to_all | solution.py:272
  99.6 34.6 %collective-permute-start = (bf16[32,16,1024]{2,1,0:T(8,128)(2,1)}, bf16[32,16,1024]{2,1,0:T(8,128)(2,1)}, u32[]{:S(2)}, u32[]{:S(2)}) collective-permute-start(bf16[32,16,1024]{2,1,0:T(8,128)(2,1)} %all_to_all.25), channel_id=1, source_target_pairs={{0,32},{32,0},{1,33},{33,1},{2,34},{34,2},{3,35},{35,3},{4,36},{36... | collective-permute-start | bytes 3145736 | tf_op jit(solution)/shard_map/ppermute | solution.py:293
  115.3 1.0 copy-start.1
where the time goes:
time: 195 us; the launch traced here: 194 us
  blocking collectives  74.7 us (38%)
  waiting for transfers between devices  43.1 us (22%)
  starting transfers between devices  40.5 us (21%)
  Pallas kernels  24.9 us (13%)
  other arithmetic  7.48 us (4%)
  local copies, waits for them, and re-layouts  2.68 us (1%)
    all_to_all x2, blocking collectives, to_all(): return lax.all_to_all(copies, axes, 0, 0, tiled=True)  49 us
    all_to_all x2, starting transfers between devices, exchange(): return lax.all_to_all(x, axes, 0, 0, tiled=True)  27.4 us
    all_to_all x1, blocking collectives, exchange(): return lax.all_to_all(x, axes, 0, 0, tiled=True)  25.7 us
    ppermute x1, waiting for transfers between devices, shards(): first_in = lax.ppermute(first_out, 'zh', swap)  23.7 us
    ppermute x1, waiting for transfers between devices, shards(): rest_in = lax.ppermute(pass_on, 'zh', swap)  12.7 us
    ppermute x1, starting transfers between devices, shards(): first_in = lax.ppermute(first_out, 'zh', swap)  7 us
    all_to_all x2, waiting for transfers between devices, exchange(): return lax.all_to_all(x, axes, 0, 0, tiled=True)  6.69 us
    pallas_call x2, Pallas kernels, pack(): pl.pallas_call(functools.partial(pack_kernel, own, [job[:2] for job in jo...  6.62 us
  transfers between devices with their start and end apart: 4, of which 3 were waited for; matrix products, arithmetic and copies ran while one was open for 4% of the time, Pallas kernels for 5%

commit v1 on v0

--- a/solution.py
+++ b/solution.py
@@ -18,7 +18,8 @@
 PAIRS = NB // 2
 TA = ("y", "zh", "x", "c")
 PLANE = ("y", "x", "c")
-FIRST = 1024
+FIRST = 512
+EACH = 768
 WIDTH = 512
 F32 = jnp.float32
 BF16 = jnp.bfloat16
@@ -102,30 +103,27 @@
 def whole_kernel(w0_ref, w1_ref, x0_ref, x1_ref, s_ref, g_ref):
     parts = (dot(w0_ref[...], rows_of(x0_ref)) + dot(w1_ref[...], rows_of(x1_ref))).astype(BF16)
     emit(parts, s_ref)
-    gram = gram_of(parts)
-
-    @pl.when(pl.program_id(0) == 0)
-    def _():
-        g_ref[...] = gram
-
-    @pl.when(pl.program_id(0) > 0)
-    def _():
-        g_ref[...] += gram
-
-
-def whole(w0, w1, x0, x1, pts):
+    g_ref[...] = gram_of(parts)
+
+
+def whole(w0, w1, x0, x1):
     times = w0.shape[1]
-    steps = x1.shape[2] // WIDTH
+    pts, count = x0.shape[2], x1.shape[2]
+    at = pts // count - 1
     fixed = pl.BlockSpec((ROWS, times), lambda i: (0, 0))
-    moving = pl.BlockSpec((*x0.shape[:2], WIDTH), lambda i: (0, 0, i))
     return pl.pallas_call(
         whole_kernel,
-        grid=(steps,),
+        grid=(1,),
         out_shape=(jax.ShapeDtypeStruct((ROWS, pts), BF16), jax.ShapeDtypeStruct((ROWS, HALF), F32)),
-        in_specs=[fixed, fixed, moving, moving],
-        out_specs=(pl.BlockSpec((ROWS, WIDTH), lambda i: (0, i)), pl.BlockSpec((ROWS, HALF), lambda i: (0, 0))),
+        in_specs=[
+            fixed,
+            fixed,
+            pl.BlockSpec((*x0.shape[:2], count), lambda i: (0, 0, at)),
+            pl.BlockSpec(x1.shape, lambda i: (0, 0, 0)),
+        ],
+        out_specs=(pl.BlockSpec((ROWS, count), lambda i: (0, at)), pl.BlockSpec((ROWS, HALF), lambda i: (0, 0))),
         compiler_params=PARAMS,
-        cost_estimate=pl.CostEstimate(flops=4 * ROWS * times * steps * WIDTH, bytes_accessed=2**22, transcendentals=0),
+        cost_estimate=pl.CostEstimate(flops=4 * ROWS * times * count, bytes_accessed=2**22, transcendentals=0),
         name="whole",
     )(w0, w1, x0, x1)
 
@@ -134,19 +132,18 @@
     p_ref[...] = dot(w_ref[...], rows_of(x_ref))
 
 
-def partial(w, x, first):
+def partial(w, x, pts):
     times = w.shape[1]
-    pts = x.shape[2] - first
-    skip = first // WIDTH
+    width = EACH // 2
     return pl.pallas_call(
         partial_kernel,
-        grid=(pts // WIDTH,),
+        grid=(pts // width,),
         out_shape=jax.ShapeDtypeStruct((ROWS, pts), F32),
         in_specs=[
             pl.BlockSpec((ROWS, times), lambda i: (0, 0)),
-            pl.BlockSpec((*x.shape[:2], WIDTH), lambda i: (0, 0, i + skip)),
+            pl.BlockSpec((*x.shape[:2], width), lambda i: (0, 0, i)),
         ],
-        out_specs=pl.BlockSpec((ROWS, WIDTH), lambda i: (0, i)),
+        out_specs=pl.BlockSpec((ROWS, width), lambda i: (0, i)),
         compiler_params=PARAMS,
         cost_estimate=pl.CostEstimate(flops=2 * ROWS * times * pts, bytes_accessed=2**21, transcendentals=0),
         name="partial",
@@ -157,55 +154,45 @@
     return lax.broadcasted_iota(jnp.int32, (rows, HALF), 1) // NF
 
 
-def rest_kernel(steps, w_ref, x_ref, p_ref, g_ref, _, s_ref, t_ref, acc):
-    step = pl.program_id(0)
+def next_kernel(w_ref, x_ref, p_ref, g_ref, _, s_ref, out_ref, last):
     parts = (p_ref[...] + dot(w_ref[...], rows_of(x_ref))).astype(BF16)
     emit(parts, s_ref)
-    gram = gram_of(parts)
-
-    @pl.when(step == 0)
-    def _():
-        acc[...] = g_ref[...] + gram
-
-    @pl.when(step > 0)
-    def _():
-        acc[...] += gram
-
-    @pl.when(step == steps - 1)
-    def _():
-        kept = jnp.where(same_freq(ROWS), acc[...], 0.0)
-        tables = kept.reshape(2 * NB, NF, HALF).sum(axis=1)
-        block = lax.broadcasted_iota(jnp.int32, (NB, HALF), 0)
-        t_ref[...] = jnp.zeros_like(t_ref)
-        for k in range(PAIRS + 1):
-            pick = (lane_block(NB) + k) % NB == block
-            t_ref[k : k + 1, :HALF] = jnp.where(pick, tables[:NB], 0.0).sum(axis=0, keepdims=True)
-            if k:
-                row = PAIRS + k
-                t_ref[row : row + 1, :HALF] = jnp.where(pick, tables[NB:], 0.0).sum(axis=0, keepdims=True)
-
-
-def rest(w, x, p, g, s):
+    total = g_ref[...] + gram_of(parts)
+    if not last:
+        out_ref[...] = total
+        return
+    kept = jnp.where(same_freq(ROWS), total, 0.0)
+    tables = kept.reshape(2 * NB, NF, HALF).sum(axis=1)
+    block = lax.broadcasted_iota(jnp.int32, (NB, HALF), 0)
+    out_ref[...] = jnp.zeros_like(out_ref)
+    for k in range(PAIRS + 1):
+        pick = (lane_block(NB) + k) % NB == block
+        out_ref[k : k + 1, :HALF] = jnp.where(pick, tables[:NB], 0.0).sum(axis=0, keepdims=True)
+        if k:
+            row = PAIRS + k
+            out_ref[row : row + 1, :HALF] = jnp.where(pick, tables[NB:], 0.0).sum(axis=0, keepdims=True)
+
+
+def next_part(at, last, w, x, p, g, s):
     times = w.shape[1]
-    steps = x.shape[2] // WIDTH
-    skip = s.shape[1] // WIDTH - steps
-    return pl.pallas_call(
-        functools.partial(rest_kernel, steps),
-        grid=(steps,),
-        out_shape=(jax.ShapeDtypeStruct(s.shape, BF16), jax.ShapeDtypeStruct((8, 256), F32)),
+    width = x.shape[2]
+    out = (8, 256) if last else (ROWS, HALF)
+    return pl.pallas_call(
+        functools.partial(next_kernel, last=last),
+        grid=(1,),
+        out_shape=(jax.ShapeDtypeStruct(s.shape, BF16), jax.ShapeDtypeStruct(out, F32)),
         in_specs=[
             pl.BlockSpec((ROWS, times), lambda i: (0, 0)),
-            pl.BlockSpec((*x.shape[:2], WIDTH), lambda i: (0, 0, i)),
-            pl.BlockSpec((ROWS, WIDTH), lambda i: (0, i)),
+            pl.BlockSpec(x.shape, lambda i: (0, 0, 0)),
+            pl.BlockSpec((ROWS, width), lambda i: (0, at)),
             pl.BlockSpec((ROWS, HALF), lambda i: (0, 0)),
             pl.BlockSpec(memory_space=pl.ANY),
         ],
-        out_specs=(pl.BlockSpec((ROWS, WIDTH), lambda i: (0, i + skip)), pl.BlockSpec((8, 256), lambda i: (0, 0))),
-        scratch_shapes=[pltpu.VMEM((ROWS, HALF), F32)],
+        out_specs=(pl.BlockSpec((ROWS, width), lambda i: (0, at)), pl.BlockSpec(out, lambda i: (0, 0))),
         input_output_aliases={4: 0},
         compiler_params=PARAMS,
-        cost_estimate=pl.CostEstimate(flops=2 * ROWS * times * steps * WIDTH, bytes_accessed=2**22, transcendentals=0),
-        name="rest",
+        cost_estimate=pl.CostEstimate(flops=2 * ROWS * times * width, bytes_accessed=2**22, transcendentals=0),
+        name="next_part",
     )(w, x, p, g, s)
 
 
@@ -280,22 +267,27 @@
     swap = [(0, 1), (1, 0)]
     x = snapshots.reshape(local, own * count)
 
-    (first_out,) = pack(x, own, [(1, 0, FIRST)])
-    first_in = lax.ppermute(first_out, "zh", swap)
-    pass_on, mine = pack(x, own, [(1, FIRST, own - FIRST), (0, 0, own)])
-    pass_on = exchange(pass_on, PLANE)
+    later = own - FIRST
+    (first,) = pack(x, own, [(1, later, FIRST)])
+    first = lax.ppermute(first, "zh", swap)
+    (part0,) = pack(x, own, [(1, 0, EACH)])
+    part0 = exchange(part0, PLANE)
+    part0 = lax.ppermute(part0, "zh", swap)
+    part1, mine = pack(x, own, [(1, EACH, EACH), (0, 0, own)])
+    part1 = exchange(part1, PLANE)
+    x0 = exchange(mine, PLANE)
     side = lax.axis_index("zh")
     place = jnp.arange(local * count // 2, dtype=jnp.int32)
     times = place // 128 * 256 + place % 128
     w0 = weights(block_starts, kept_freqs, times + side * 128)
     w1 = weights(block_starts, kept_freqs, times + (1 - side) * 128)
-    pass_on, w0, w1 = lax.optimization_barrier((pass_on, w0, w1))
-    rest_in = lax.ppermute(pass_on, "zh", swap)
-    x0 = exchange(mine, PLANE)
-    x1 = exchange(first_in, PLANE)
-    s, g = whole(w0, w1, x0, x1, own)
-    p = partial(w0, x0, FIRST)
-    s, t = rest(w1, rest_in, p, g, s)
+    part1, w0, w1 = lax.optimization_barrier((part1, w0, w1))
+    part1 = lax.ppermute(part1, "zh", swap)
+    first = exchange(first, PLANE)
+    p = partial(w0, x0, later)
+    s, g = whole(w0, w1, x0, first)
+    s, g = next_part(0, False, w1, part0, p, g, s)
+    s, t = next_part(1, True, w1, part1, p, g, s)
     t = to_all(t, ("y", "x")).sum(axis=0)
     t = to_all(t, ("zh", "zl", "c"))
     out = power(t, s, float(NB * total))

time: 195 us -> 210 us (1.077)
  waiting for transfers between devices: 43.1 us -> 52.5 us
  Pallas kernels: 24.9 us -> 29.8 us
  blocking collectives: 74.7 us -> 78.9 us
  starting transfers between devices: 40.5 us -> 38.3 us
    all_to_all x2 -> x3, waiting for transfers between devices: 6.69 us -> 21 us  [exchange(): return lax.all_to_all(x, axes, 0, 0, tiled=True)]
    all_to_all x2, blocking collectives: 49 us -> 59.4 us  [to_all(): return lax.all_to_all(copies, axes, 0, 0, tiled=True)]
    all_to_all x2 -> x3, starting transfers between devices: 27.4 us -> 17.5 us  [exchange(): return lax.all_to_all(x, axes, 0, 0, tiled=True)]
    ppermute x2 -> x3, starting transfers between devices: 13 us -> 20.7 us  [the longest x1 13.7 us: shards(): part0 = lax.ppermute(part0, 'zh', swap)]
    all_to_all x1, blocking collectives: 25.7 us -> 19.5 us  [exchange(): return lax.all_to_all(x, axes, 0, 0, tiled=True)]
    ppermute x2 -> x3, waiting for transfers between devices: 36.4 us -> 31.6 us  [the longest x1 16.9 us: shards(): part1 = lax.ppermute(part1, 'zh', swap)]
    pallas_call x3 -> x4, Pallas kernels: 12.8 us -> 16 us  [the longest x2 7.72 us: next_part(): pl.pallas_call(functools.partial(next_kernel, last=last), grid=(1,), out_...]
    pallas_call x2 -> x3, Pallas kernels: 6.62 us -> 8.34 us  [pack(): pl.pallas_call(functools.partial(pack_kernel, own, [job[:2] for job in jo...]
  transfers between devices with their start and end apart: 4 -> 6, of which waited for: 3 -> 5; matrix products, arithmetic and copies ran while one was open for 4% -> 3% of each run, Pallas kernels for 5% -> 8%
where the time goes in v1:
time: 210 us; the launch traced here: 209 us
  blocking collectives  78.9 us (38%)
  waiting for transfers between devices  52.5 us (25%)
  starting transfers between devices  38.3 us (18%)
  Pallas kernels  29.8 us (14%)
  other arithmetic  5.92 us (3%)
  local copies, waits for them, and re-layouts  2.96 us (1%)
    all_to_all x2, blocking collectives, to_all(): return lax.all_to_all(copies, axes, 0, 0, tiled=True)  59.4 us
    all_to_all x3, waiting for transfers between devices, exchange(): return lax.all_to_all(x, axes, 0, 0, tiled=True)  21 us
    all_to_all x1, blocking collectives, exchange(): return lax.all_to_all(x, axes, 0, 0, tiled=True)  19.5 us
    all_to_all x3, starting transfers between devices, exchange(): return lax.all_to_all(x, axes, 0, 0, tiled=True)  17.5 us
    ppermute x1, waiting for transfers between devices, shards(): part1 = lax.ppermute(part1, 'zh', swap)  16.9 us
    ppermute x1, waiting for transfers between devices, shards(): first = lax.ppermute(first, 'zh', swap)  14.2 us
    ppermute x1, starting transfers between devices, shards(): part0 = lax.ppermute(part0, 'zh', swap)  13.7 us
    pallas_call x3, Pallas kernels, pack(): pl.pallas_call(functools.partial(pack_kernel, own, [job[:2] for job in jo...  8.34 us
  transfers between devices with their start and end apart: 6, of which 5 were waited for; matrix products, arithmetic and copies ran while one was open for 3% of the time, Pallas kernels for 8%

profile of v1, /device:TPU:1, one launch (start us, length us, event | category | flops | bytes accessed | tf_op | source)
XLA Modules:
  0.0 209.2 jit_solution(17936014143630244906)
XLA Ops:
  0.6 4.0 %pack.3 = (bf16[32,16,768]{2,1,0:T(8,128)(2,1)}, bf16[32,16,2048]{2,1,0:T(8,128)(2,1)}) custom-call(bf16[16,131072]{1,0:T(8,128)(2,1)} %bitcast.5), custom_call_target="tpu_custom_call" | custom-call | tf_op jit(solution)/shard_map/pack/pallas_call | solution.py:76
  4.6 8.6 %all-to-all-start = ((bf16[32,16,768]{2,1,0:T(8,128)(2,1)}), bf16[32,16,768]{2,1,0:T(8,128)(2,1)S(1)}, u32[]{:S(2)}, u32[]{:S(2)}) async-start(bf16[32,16,768]{2,1,0:T(8,128)(2,1)} %get-tuple-element.13), calls=%async_computation | async-start | bytes 1572864 | tf_op jit(solution)/shard_map/all_to_all | solution.py:259
  13.2 2.3 %pack.4 = bf16[32,16,768]{2,1,0:T(8,128)(2,1)} custom-call(bf16[16,131072]{1,0:T(8,128)(2,1)} %bitcast.6), custom_call_target="tpu_custom_call" | custom-call | tf_op jit(solution)/shard_map/pack/pallas_call | solution.py:76
  15.5 12.0 %all-to-all-done = bf16[32,16,768]{2,1,0:T(8,128)(2,1)S(1)} async-done(((bf16[32,16,768]{2,1,0:T(8,128)(2,1)}), bf16[32,16,768]{2,1,0:T(8,128)(2,1)S(1)}, u32[]{:S(2)}, u32[]{:S(2)}) %all-to-all-start) | async-done | bytes 786464 | tf_op jit(solution)/shard_map/all_to_all | solution.py:259
  27.4 4.7 %all-to-all-start.2 = ((bf16[32,16,768]{2,1,0:T(8,128)(2,1)}), bf16[32,16,768]{2,1,0:T(8,128)(2,1)}, u32[]{:S(2)}, u32[]{:S(2)}) async-start(bf16[32,16,768]{2,1,0:T(8,128)(2,1)} %pack.4), calls=%async_computation.2 | async-start | bytes 1572864 | tf_op jit(solution)/shard_map/all_to_all | solution.py:259
  32.2 2.1 pack.5
  34.3 7.0 %collective-permute-start.2 = (bf16[32,16,512]{2,1,0:T(8,128)(2,1)}, bf16[32,16,512]{2,1,0:T(8,128)(2,1)S(1)}, u32[]{:S(2)}, u32[]{:S(2)}) collective-permute-start(bf16[32,16,512]{2,1,0:T(8,128)(2,1)} %pack.5), channel_id=1, source_target_pairs={{0,32},{32,0},{1,33},{33,1},{2,34},{34,2},{3,35},{35,3},{4,36},{36... | collective-permute-start | bytes 1572872 | tf_op jit(solution)/shard_map/ppermute | solution.py:272
  41.3 14.2 %collective-permute-done.2 = bf16[32,16,512]{2,1,0:T(8,128)(2,1)S(1)} collective-permute-done((bf16[32,16,512]{2,1,0:T(8,128)(2,1)}, bf16[32,16,512]{2,1,0:T(8,128)(2,1)S(1)}, u32[]{:S(2)}, u32[]{:S(2)}) %collective-permute-start.2) | collective-permute-done | bytes 524320 | tf_op jit(solution)/shard_map/ppermute | solution.py:272
  55.5 0.0 all-to-all-done.2
  55.5 19.5 %all_to_all.30.x1_ref = bf16[32,16,512]{2,1,0:T(8,128)(2,1)} all-to-all(bf16[32,16,512]{2,1,0:T(8,128)(2,1)S(1)} %collective-permute-done.2), channel_id=1, replica_groups=mesh['y'=4,'zh'=2,'x'=4,'c'=2,'zl'=4] {'y','x','c'}, dimensions={0} | all-to-all | bytes 1048576 | tf_op jit(solution)/shard_map/all_to_all | solution.py:259
  75.1 4.2 %all-to-all-start.1 = ((bf16[32,16,2048]{2,1,0:T(8,128)(2,1)}), bf16[32,16,2048]{2,1,0:T(8,128)(2,1)S(1)}, u32[]{:S(2)}, u32[]{:S(2)}) async-start(bf16[32,16,2048]{2,1,0:T(8,128)(2,1)} %get-tuple-element.17), calls=%async_computation.1 | async-start | bytes 4194304 | tf_op jit(solution)/shard_map/all_to_all | solution.py:259
  79.3 0.0 copy-done.3
  79.3 0.1 subtract_select_fusion
  79.4 0.2 fusion.15
  79.6 4.0 %multiply_convert_fusion.1 = (bf16[1,7,32,512]{3,2,1,0:T(8,128)(2,1)S(1)}, bf16[1,7,32,512]{3,2,1,0:T(8,128)(2,1)S(1)}, bf16[1,7,32,512]{3,2,1,0:T(8,128)(2,1)S(1)}, bf16[1,7,32,512]{3,2,1,0:T(8,128)(2,1)S(1)}) fusion(f32[7,512]{1,0:T(8,128)S(1)} %get-tuple-element.28, s32[7,512]{1,0:T(8,128)S(1)} %get-tuple-element.36, s32[32]{0:T(128)S(1)} %copy-done.4, ...), kind=kLoop, calls=%fused_computation.19 | loop fusion | flops 4587520 | bytes 1003648 | tf_op jit(solution)/shard_map/convert
  83.5 0.8 pad_maximum_fusion
  84.4 13.7 %collective-permute-start.1 = (bf16[32,16,768]{2,1,0:T(8,128)(2,1)}, bf16[32,16,768]{2,1,0:T(8,128)(2,1)}, u32[]{:S(2)}, u32[]{:S(2)}) collective-permute-start(bf16[32,16,768]{2,1,0:T(8,128)(2,1)} %all-to-all-done.2), channel_id=1, source_target_pairs={{0,32},{32,0},{1,33},{33,1},{2,34},{34,2},{3,35},{35,3},{4,36},{36... | collective-permute-start | bytes 2359304 | tf_op jit(solution)/shard_map/ppermute | solution.py:275
  98.1 0.8 pad_maximum_fusion.1
  99.0 0.0 collective-permute-start
  99.0 9.0 %all-to-all-done.1.x_ref.x0_ref = bf16[32,16,2048]{2,1,0:T(8,128)(2,1)S(1)} async-done(((bf16[32,16,2048]{2,1,0:T(8,128)(2,1)}), bf16[32,16,2048]{2,1,0:T(8,128)(2,1)S(1)}, u32[]{:S(2)}, u32[]{:S(2)}) %all-to-all-start.1) | async-done | bytes 2097184 | tf_op jit(solution)/shard_map/all_to_all | solution.py:259
  108.0 1.3 copy-done
  109.3 3.6 %whole.1 = (bf16[448,2048]{1,0:T(8,128)(2,1)}, f32[448,224]{1,0:T(8,128)}) custom-call(bf16[448,512]{1,0:T(8,128)(2,1)} %bitcast.12, bf16[448,512]{1,0:T(8,128)(2,1)} %bitcast.9, bf16[32,16,2048]{2,1,0:T(8,128)(2,1)} %copy-done, bf16[32,16,512]{2,1,0:T(8,128)(2,1)} %all_to_all.30.x1_ref), custom_call_target="tpu_custom_call" | custom-call | flops 469762048 | bytes 4194304 | tf_op jit(solution)/shard_map/whole/pallas_call | solution.py:114
  112.9 4.7 %partial.1.p_ref = f32[448,1536]{1,0:T(8,128)} custom-call(bf16[448,512]{1,0:T(8,128)(2,1)} %bitcast.13, bf16[32,16,2048]{2,1,0:T(8,128)(2,1)} %copy-done), custom_call_target="tpu_custom_call" | custom-call | flops 704643072 | bytes 2097152 | tf_op jit(solution)/shard_map/partial/pallas_call | solution.py:138
  117.6 0.5 collective-permute-done.1.x_ref
  118.1 3.9 %next_part.2 = (bf16[448,2048]{1,0:T(8,128)(2,1)}, f32[448,224]{1,0:T(8,128)}) custom-call(bf16[448,512]{1,0:T(8,128)(2,1)} %bitcast.10, bf16[32,16,768]{2,1,0:T(8,128)(2,1)} %collective-permute-done.1.x_ref, f32[448,1536]{1,0:T(8,128)} %partial.1.p_ref, f32[448,224]{1,0:T(8,128)} %get-tuple-element.18.g_ref, ...), custom_call_target="tpu_custom_call", output_to_operand_aliasing={{0}: (4, {})} | custom-call | flops 352321536 | bytes 4194304 | tf_op jit(solution)/shard_map/next_part/pallas_call | solution.py:180
  122.0 16.9 %collective-permute-done.x_ref = bf16[32,16,768]{2,1,0:T(8,128)(2,1)S(1)} collective-permute-done((bf16[32,16,768]{2,1,0:T(8,128)(2,1)}, bf16[32,16,768]{2,1,0:T(8,128)(2,1)S(1)}, u32[]{:S(2)}, u32[]{:S(2)}) %collective-permute-start) | collective-permute-done | bytes 786464 | tf_op jit(solution)/shard_map/ppermute | solution.py:285
  138.9 0.9 copy-done.1
  139.8 3.8 %next_part.3 = (bf16[448,2048]{1,0:T(8,128)(2,1)}, f32[8,256]{1,0:T(8,128)}) custom-call(bf16[448,512]{1,0:T(8,128)(2,1)} %bitcast.11, bf16[32,16,768]{2,1,0:T(8,128)(2,1)} %copy-done.1, f32[448,1536]{1,0:T(8,128)} %partial.1.p_ref, f32[448,224]{1,0:T(8,128)} %get-tuple-element.20.g_ref, ...), custom_call_target="tpu_custom_call", output_to_operand_aliasing={{0}: (4, {})} | custom-call | flops 352321536 | bytes 4194304 | tf_op jit(solution)/shard_map/next_part/pallas_call | solution.py:180
  143.5 0.7 broadcast_in_dim.13
  144.3 13.4 %all_to_all.31 = f32[16,8,256]{2,1,0:T(8,128)S(1)} all-to-all(f32[16,8,256]{2,1,0:T(8,128)S(1)} %broadcast_in_dim.13), channel_id=1, replica_groups=mesh['y'=4,'zh'=2,'x'=4,'c'=2,'zl'=4] {'y','x'}, dimensions={0} | all-to-all | bytes 262144 | tf_op jit(solution)/shard_map/all_to_all | solution.py:255
  157.7 46.0 %all_to_all.32.t_ref = f32[16,8,256]{2,1,0:T(8,128)} all-to-all(f32[16,8,256]{2,1,0:T(8,128)S(1)} %broadcast_in_dim.14), channel_id=1, replica_groups=mesh['y'=4,'zh'=2,'x'=4,'c'=2,'zl'=4] {'zh','zl','c'}, dimensions={0} | all-to-all | bytes 262144 | tf_op jit(solution)/shard_map/all_to_all | solution.py:255
  203.7 5.5 %power.1 = f32[448,2048]{1,0:T(8,128)} custom-call(f32[16,8,256]{2,1,0:T(8,128)} %all_to_all.32.t_ref, bf16[448,2048]{1,0:T(8,128)(2,1)} %get-tuple-element.22.s_ref), custom_call_target="tpu_custom_call" | custom-call | tf_op jit(solution)/shard_map/power/pallas_call | solution.py:238
  (10 shorter events, 0.0 us)
Async XLA Ops:
  4.6 22.8 %all-to-all-start = ((bf16[32,16,768]{2,1,0:T(8,128)(2,1)}), bf16[32,16,768]{2,1,0:T(8,128)(2,1)S(1)}, u32[]{:S(2)}, u32[]{:S(2)}) async-start(bf16[32,16,768]{2,1,0:T(8,128)(2,1)} %get-tuple-element.13), calls=%async_computation | async-start | bytes 1572864 | tf_op jit(solution)/shard_map/all_to_all | solution.py:259
  27.4 6.8 %copy-start.2 = (bf16[32,16,768]{2,1,0:T(8,128)(2,1)}, bf16[32,16,768]{2,1,0:T(8,128)(2,1)S(1)}, u32[]{:S(2)}) copy-start(bf16[32,16,768]{2,1,0:T(8,128)(2,1)S(1)} %all-to-all-done) | copy-start | bytes 2359300
  27.4 28.1 %all-to-all-start.2 = ((bf16[32,16,768]{2,1,0:T(8,128)(2,1)}), bf16[32,16,768]{2,1,0:T(8,128)(2,1)}, u32[]{:S(2)}, u32[]{:S(2)}) async-start(bf16[32,16,768]{2,1,0:T(8,128)(2,1)} %pack.4), calls=%async_computation.2 | async-start | bytes 1572864 | tf_op jit(solution)/shard_map/all_to_all | solution.py:259
  34.3 21.2 %collective-permute-start.2 = (bf16[32,16,512]{2,1,0:T(8,128)(2,1)}, bf16[32,16,512]{2,1,0:T(8,128)(2,1)S(1)}, u32[]{:S(2)}, u32[]{:S(2)}) collective-permute-start(bf16[32,16,512]{2,1,0:T(8,128)(2,1)} %pack.5), channel_id=1, source_target_pairs={{0,32},{32,0},{1,33},{33,1},{2,34},{34,2},{3,35},{35,3},{4,36},{36... | collective-permute-start | bytes 1572872 | tf_op jit(solution)/shard_map/ppermute | solution.py:272
  75.1 4.2 %copy-start.3 = (s32[7]{0:T(128)S(1)}, s32[7]{0:T(128)}, u32[]{:S(2)}) copy-start(s32[7]{0:T(128)} %param.4) | copy-start | bytes 88
  75.1 4.5 %copy-start.4 = (s32[32]{0:T(128)S(1)}, s32[32]{0:T(128)}, u32[]{:S(2)}) copy-start(s32[32]{0:T(128)} %param.5) | copy-start | bytes 388
  75.1 32.9 %all-to-all-start.1 = ((bf16[32,16,2048]{2,1,0:T(8,128)(2,1)}), bf16[32,16,2048]{2,1,0:T(8,128)(2,1)S(1)}, u32[]{:S(2)}, u32[]{:S(2)}) async-start(bf16[32,16,2048]{2,1,0:T(8,128)(2,1)} %get-tuple-element.17), calls=%async_computation.1 | async-start | bytes 4194304 | tf_op jit(solution)/shard_map/all_to_all | solution.py:259
  84.4 33.7 %collective-permute-start.1 = (bf16[32,16,768]{2,1,0:T(8,128)(2,1)}, bf16[32,16,768]{2,1,0:T(8,128)(2,1)}, u32[]{:S(2)}, u32[]{:S(2)}) collective-permute-start(bf16[32,16,768]{2,1,0:T(8,128)(2,1)} %all-to-all-done.2), channel_id=1, source_target_pairs={{0,32},{32,0},{1,33},{33,1},{2,34},{34,2},{3,35},{35,3},{4,36},{36... | collective-permute-start | bytes 2359304 | tf_op jit(solution)/shard_map/ppermute | solution.py:275
  99.0 39.9 %collective-permute-start = (bf16[32,16,768]{2,1,0:T(8,128)(2,1)}, bf16[32,16,768]{2,1,0:T(8,128)(2,1)S(1)}, u32[]{:S(2)}, u32[]{:S(2)}) collective-permute-start(bf16[32,16,768]{2,1,0:T(8,128)(2,1)} %copy-done.2), channel_id=1, source_target_pairs={{0,32},{32,0},{1,33},{33,1},{2,34},{34,2},{3,35},{35,3},{4,36},{36... | collective-permute-start | bytes 2359304 | tf_op jit(solution)/shard_map/ppermute | solution.py:285
  108.0 1.3 copy-start
  138.9 0.9 copy-start.1

commit v2 on v0

--- a/solution.py
+++ b/solution.py
@@ -18,7 +18,7 @@
 PAIRS = NB // 2
 TA = ("y", "zh", "x", "c")
 PLANE = ("y", "x", "c")
-FIRST = 1024
+FIRST = 768
 WIDTH = 512
 F32 = jnp.float32
 BF16 = jnp.bfloat16
@@ -113,19 +113,24 @@
         g_ref[...] += gram
 
 
-def whole(w0, w1, x0, x1, pts):
+def whole(w0, w1, x0, x1, width):
     times = w0.shape[1]
-    steps = x1.shape[2] // WIDTH
+    pts, count = x0.shape[2], x1.shape[2]
+    skip = (pts - count) // width
     fixed = pl.BlockSpec((ROWS, times), lambda i: (0, 0))
-    moving = pl.BlockSpec((*x0.shape[:2], WIDTH), lambda i: (0, 0, i))
     return pl.pallas_call(
         whole_kernel,
-        grid=(steps,),
+        grid=(count // width,),
         out_shape=(jax.ShapeDtypeStruct((ROWS, pts), BF16), jax.ShapeDtypeStruct((ROWS, HALF), F32)),
-        in_specs=[fixed, fixed, moving, moving],
-        out_specs=(pl.BlockSpec((ROWS, WIDTH), lambda i: (0, i)), pl.BlockSpec((ROWS, HALF), lambda i: (0, 0))),
+        in_specs=[
+            fixed,
+            fixed,
+            pl.BlockSpec((*x0.shape[:2], width), lambda i: (0, 0, i + skip)),
+            pl.BlockSpec((*x0.shape[:2], width), lambda i: (0, 0, i)),
+        ],
+        out_specs=(pl.BlockSpec((ROWS, width), lambda i: (0, i + skip)), pl.BlockSpec((ROWS, HALF), lambda i: (0, 0))),
         compiler_params=PARAMS,
-        cost_estimate=pl.CostEstimate(flops=4 * ROWS * times * steps * WIDTH, bytes_accessed=2**22, transcendentals=0),
+        cost_estimate=pl.CostEstimate(flops=4 * ROWS * times * count, bytes_accessed=2**22, transcendentals=0),
         name="whole",
     )(w0, w1, x0, x1)
 
@@ -134,19 +139,17 @@
     p_ref[...] = dot(w_ref[...], rows_of(x_ref))
 
 
-def partial(w, x, first):
+def partial(w, x, pts, width):
     times = w.shape[1]
-    pts = x.shape[2] - first
-    skip = first // WIDTH
     return pl.pallas_call(
         partial_kernel,
-        grid=(pts // WIDTH,),
+        grid=(pts // width,),
         out_shape=jax.ShapeDtypeStruct((ROWS, pts), F32),
         in_specs=[
             pl.BlockSpec((ROWS, times), lambda i: (0, 0)),
-            pl.BlockSpec((*x.shape[:2], WIDTH), lambda i: (0, 0, i + skip)),
+            pl.BlockSpec((*x.shape[:2], width), lambda i: (0, 0, i)),
         ],
-        out_specs=pl.BlockSpec((ROWS, WIDTH), lambda i: (0, i)),
+        out_specs=pl.BlockSpec((ROWS, width), lambda i: (0, i)),
         compiler_params=PARAMS,
         cost_estimate=pl.CostEstimate(flops=2 * ROWS * times * pts, bytes_accessed=2**21, transcendentals=0),
         name="partial",
@@ -185,26 +188,25 @@
                 t_ref[row : row + 1, :HALF] = jnp.where(pick, tables[NB:], 0.0).sum(axis=0, keepdims=True)
 
 
-def rest(w, x, p, g, s):
+def rest(w, x, p, g, s, width):
     times = w.shape[1]
-    steps = x.shape[2] // WIDTH
-    skip = s.shape[1] // WIDTH - steps
+    steps = x.shape[2] // width
     return pl.pallas_call(
         functools.partial(rest_kernel, steps),
         grid=(steps,),
         out_shape=(jax.ShapeDtypeStruct(s.shape, BF16), jax.ShapeDtypeStruct((8, 256), F32)),
         in_specs=[
             pl.BlockSpec((ROWS, times), lambda i: (0, 0)),
-            pl.BlockSpec((*x.shape[:2], WIDTH), lambda i: (0, 0, i)),
-            pl.BlockSpec((ROWS, WIDTH), lambda i: (0, i)),
+            pl.BlockSpec((*x.shape[:2], width), lambda i: (0, 0, i)),
+            pl.BlockSpec((ROWS, width), lambda i: (0, i)),
             pl.BlockSpec((ROWS, HALF), lambda i: (0, 0)),
             pl.BlockSpec(memory_space=pl.ANY),
         ],
-        out_specs=(pl.BlockSpec((ROWS, WIDTH), lambda i: (0, i + skip)), pl.BlockSpec((8, 256), lambda i: (0, 0))),
+        out_specs=(pl.BlockSpec((ROWS, width), lambda i: (0, i)), pl.BlockSpec((8, 256), lambda i: (0, 0))),
         scratch_shapes=[pltpu.VMEM((ROWS, HALF), F32)],
         input_output_aliases={4: 0},
         compiler_params=PARAMS,
-        cost_estimate=pl.CostEstimate(flops=2 * ROWS * times * steps * WIDTH, bytes_accessed=2**22, transcendentals=0),
+        cost_estimate=pl.CostEstimate(flops=2 * ROWS * times * x.shape[2], bytes_accessed=2**22, transcendentals=0),
         name="rest",
     )(w, x, p, g, s)
 
@@ -280,22 +282,24 @@
     swap = [(0, 1), (1, 0)]
     x = snapshots.reshape(local, own * count)
 
-    (first_out,) = pack(x, own, [(1, 0, FIRST)])
-    first_in = lax.ppermute(first_out, "zh", swap)
-    pass_on, mine = pack(x, own, [(1, FIRST, own - FIRST), (0, 0, own)])
+    later = own - FIRST
+    (first,) = pack(x, own, [(1, later, FIRST)])
+    first = lax.ppermute(first, "zh", swap)
+    (pass_on,) = pack(x, own, [(1, 0, later)])
     pass_on = exchange(pass_on, PLANE)
+    passed = lax.ppermute(pass_on, "zh", swap)
+    (mine,) = pack(x, own, [(0, 0, own)])
+    x0 = exchange(mine, PLANE)
     side = lax.axis_index("zh")
     place = jnp.arange(local * count // 2, dtype=jnp.int32)
     times = place // 128 * 256 + place % 128
     w0 = weights(block_starts, kept_freqs, times + side * 128)
     w1 = weights(block_starts, kept_freqs, times + (1 - side) * 128)
-    pass_on, w0, w1 = lax.optimization_barrier((pass_on, w0, w1))
-    rest_in = lax.ppermute(pass_on, "zh", swap)
-    x0 = exchange(mine, PLANE)
-    x1 = exchange(first_in, PLANE)
-    s, g = whole(w0, w1, x0, x1, own)
-    p = partial(w0, x0, FIRST)
-    s, t = rest(w1, rest_in, p, g, s)
+    first, w0, w1 = lax.optimization_barrier((first, w0, w1))
+    first = exchange(first, PLANE)
+    p = partial(w0, x0, later, 640)
+    s, g = whole(w0, w1, x0, first, 256)
+    s, t = rest(w1, passed, p, g, s, 640)
     t = to_all(t, ("y", "x")).sum(axis=0)
     t = to_all(t, ("zh", "zl", "c"))
     out = power(t, s, float(NB * total))

time: 195 us -> 181 us (0.928)
  blocking collectives: 74.7 us -> 60.1 us
  starting transfers between devices: 40.5 us -> 30.9 us
  waiting for transfers between devices: 43.1 us -> 52 us
  Pallas kernels: 24.9 us -> 27.5 us
    all_to_all x1 -> x0, blocking collectives: 25.7 us -> none  [exchange(): return lax.all_to_all(x, axes, 0, 0, tiled=True)]
    all_to_all x2 -> x3, waiting for transfers between devices: 6.69 us -> 27.2 us  [exchange(): return lax.all_to_all(x, axes, 0, 0, tiled=True)]
    ppermute x2, waiting for transfers between devices: 36.4 us -> 24.8 us  [the longest x1 15.1 us: shards(): first = lax.ppermute(first, 'zh', swap)]
    all_to_all x2, blocking collectives: 49 us -> 60.1 us  [to_all(): return lax.all_to_all(copies, axes, 0, 0, tiled=True)]
    ppermute x2, starting transfers between devices: 13 us -> 7.12 us  [the longest x1 7 us: shards(): first = lax.ppermute(first, 'zh', swap)]
    all_to_all x2 -> x3, starting transfers between devices: 27.4 us -> 23.8 us  [exchange(): return lax.all_to_all(x, axes, 0, 0, tiled=True)]
    pallas_call x2 -> x3, Pallas kernels: 6.62 us -> 8.1 us  [pack(): pl.pallas_call(functools.partial(pack_kernel, own, [job[:2] for job in jo...]
  transfers between devices with their start and end apart: 4 -> 5, of which waited for: 3 -> 4; matrix products, arithmetic and copies ran while one was open for 4% -> 3% of each run, Pallas kernels for 5% -> 8%
where the time goes in v2:
time: 181 us; the launch traced here: 180 us
  blocking collectives  60.1 us (33%)
  waiting for transfers between devices  52 us (29%)
  starting transfers between devices  30.9 us (17%)
  Pallas kernels  27.5 us (15%)
  other arithmetic  5.88 us (3%)
  local copies, waits for them, and re-layouts  2.51 us (1%)
    all_to_all x2, blocking collectives, to_all(): return lax.all_to_all(copies, axes, 0, 0, tiled=True)  60.1 us
    all_to_all x3, waiting for transfers between devices, exchange(): return lax.all_to_all(x, axes, 0, 0, tiled=True)  27.2 us
    all_to_all x3, starting transfers between devices, exchange(): return lax.all_to_all(x, axes, 0, 0, tiled=True)  23.8 us
    ppermute x1, waiting for transfers between devices, shards(): first = lax.ppermute(first, 'zh', swap)  15.1 us
    ppermute x1, waiting for transfers between devices, shards(): passed = lax.ppermute(pass_on, 'zh', swap)  9.71 us
    pallas_call x3, Pallas kernels, pack(): pl.pallas_call(functools.partial(pack_kernel, own, [job[:2] for job in jo...  8.1 us
    ppermute x1, starting transfers between devices, shards(): first = lax.ppermute(first, 'zh', swap)  7 us
    pallas_call x1, Pallas kernels, power(): pl.pallas_call(functools.partial(power_kernel, denominator), grid=(pts //...  5.5 us
  transfers between devices with their start and end apart: 5, of which 4 were waited for; matrix products, arithmetic and copies ran while one was open for 3% of the time, Pallas kernels for 8%

profile of v2, /device:TPU:1, one launch (start us, length us, event | category | flops | bytes accessed | tf_op | source)
XLA Modules:
  0.0 179.7 jit_solution(3972362936509146887)
XLA Ops:
  0.6 2.6 %pack.4 = bf16[32,16,1280]{2,1,0:T(8,128)(2,1)} custom-call(bf16[16,131072]{1,0:T(8,128)(2,1)} %bitcast.5), custom_call_target="tpu_custom_call" | custom-call | tf_op jit(solution)/shard_map/pack/pallas_call | solution.py:75
  3.3 8.6 %all-to-all-start = ((bf16[32,16,1280]{2,1,0:T(8,128)(2,1)}), bf16[32,16,1280]{2,1,0:T(8,128)(2,1)}, u32[]{:S(2)}, u32[]{:S(2)}) async-start(bf16[32,16,1280]{2,1,0:T(8,128)(2,1)} %pack.4), calls=%async_computation | async-start | bytes 2621440 | tf_op jit(solution)/shard_map/all_to_all | solution.py:274
  11.9 3.2 %pack.5 = bf16[32,16,2048]{2,1,0:T(8,128)(2,1)} custom-call(bf16[16,131072]{1,0:T(8,128)(2,1)} %bitcast.6), custom_call_target="tpu_custom_call" | custom-call | tf_op jit(solution)/shard_map/pack/pallas_call | solution.py:75
  15.1 16.1 %all-to-all-done = bf16[32,16,1280]{2,1,0:T(8,128)(2,1)} async-done(((bf16[32,16,1280]{2,1,0:T(8,128)(2,1)}), bf16[32,16,1280]{2,1,0:T(8,128)(2,1)}, u32[]{:S(2)}, u32[]{:S(2)}) %all-to-all-start) | async-done | bytes 1310752 | tf_op jit(solution)/shard_map/all_to_all | solution.py:274
  31.3 5.2 %all-to-all-start.1 = ((bf16[32,16,2048]{2,1,0:T(8,128)(2,1)}), bf16[32,16,2048]{2,1,0:T(8,128)(2,1)S(1)}, u32[]{:S(2)}, u32[]{:S(2)}) async-start(bf16[32,16,2048]{2,1,0:T(8,128)(2,1)} %pack.5), calls=%async_computation.1 | async-start | bytes 4194304 | tf_op jit(solution)/shard_map/all_to_all | solution.py:274
  36.4 0.0 copy-start.3
  36.4 0.0 copy-start.4
  36.5 2.3 %pack.3 = bf16[32,16,768]{2,1,0:T(8,128)(2,1)} custom-call(bf16[16,131072]{1,0:T(8,128)(2,1)} %bitcast.7), custom_call_target="tpu_custom_call" | custom-call | tf_op jit(solution)/shard_map/pack/pallas_call | solution.py:75
  38.7 7.0 %collective-permute-start = (bf16[32,16,768]{2,1,0:T(8,128)(2,1)}, bf16[32,16,768]{2,1,0:T(8,128)(2,1)S(1)}, u32[]{:S(2)}, u32[]{:S(2)}) collective-permute-start(bf16[32,16,768]{2,1,0:T(8,128)(2,1)} %pack.3), channel_id=1, source_target_pairs={{0,32},{32,0},{1,33},{33,1},{2,34},{34,2},{3,35},{35,3},{4,36},{36... | collective-permute-start | bytes 2359304 | tf_op jit(solution)/shard_map/ppermute | solution.py:287
  45.7 0.0 copy-done.3
  45.7 0.1 subtract_select_fusion
  45.8 0.2 fusion.15
  46.0 0.1 collective-permute-start.1
  46.1 0.0 copy-done.4
  46.1 3.9 %multiply_convert_fusion.1 = (bf16[1,7,32,512]{3,2,1,0:T(8,128)(2,1)S(1)}, bf16[1,7,32,512]{3,2,1,0:T(8,128)(2,1)S(1)}, bf16[1,7,32,512]{3,2,1,0:T(8,128)(2,1)S(1)}, bf16[1,7,32,512]{3,2,1,0:T(8,128)(2,1)S(1)}) fusion(f32[7,512]{1,0:T(8,128)S(1)} %get-tuple-element.20, s32[7,512]{1,0:T(8,128)S(1)} %get-tuple-element.28, s32[32]{0:T(128)S(1)} %copy-done.4, ...), kind=kLoop, calls=%fused_computation.19 | loop fusion | flops 4587520 | bytes 1003648 | tf_op jit(solution)/shard_map/convert
  50.1 0.8 pad_maximum_fusion.1
  50.9 0.8 pad_maximum_fusion
  51.7 15.1 %collective-permute-done = bf16[32,16,768]{2,1,0:T(8,128)(2,1)S(1)} collective-permute-done((bf16[32,16,768]{2,1,0:T(8,128)(2,1)}, bf16[32,16,768]{2,1,0:T(8,128)(2,1)S(1)}, u32[]{:S(2)}, u32[]{:S(2)}) %collective-permute-start) | collective-permute-done | bytes 786464 | tf_op jit(solution)/shard_map/ppermute | solution.py:287
  66.9 0.9 copy-done.2
  67.7 0.0 all-to-all-done.1.x_ref.x0_ref
  67.7 10.0 %all-to-all-start.2 = ((bf16[32,16,768]{2,1,0:T(8,128)(2,1)}), bf16[32,16,768]{2,1,0:T(8,128)(2,1)S(1)}, u32[]{:S(2)}, u32[]{:S(2)}) async-start(bf16[32,16,768]{2,1,0:T(8,128)(2,1)} %copy-done.2), calls=%async_computation.2 | async-start | bytes 1572864 | tf_op jit(solution)/shard_map/all_to_all | solution.py:274
  77.8 0.0 copy-done
  77.8 3.3 %partial.1.p_ref = f32[448,1280]{1,0:T(8,128)} custom-call(bf16[448,512]{1,0:T(8,128)(2,1)} %bitcast.11, bf16[32,16,2048]{2,1,0:T(8,128)(2,1)} %copy-done), custom_call_target="tpu_custom_call" | custom-call | flops 587202560 | bytes 2097152 | tf_op jit(solution)/shard_map/partial/pallas_call | solution.py:144
  81.1 11.1 %all-to-all-done.2.x1_ref = bf16[32,16,768]{2,1,0:T(8,128)(2,1)S(1)} async-done(((bf16[32,16,768]{2,1,0:T(8,128)(2,1)}), bf16[32,16,768]{2,1,0:T(8,128)(2,1)S(1)}, u32[]{:S(2)}, u32[]{:S(2)}) %all-to-all-start.2) | async-done | bytes 786464 | tf_op jit(solution)/shard_map/all_to_all | solution.py:274
  92.1 0.9 copy-done.1
  93.0 5.1 %whole.1 = (bf16[448,2048]{1,0:T(8,128)(2,1)}, f32[448,224]{1,0:T(8,128)}) custom-call(bf16[448,512]{1,0:T(8,128)(2,1)} %bitcast.12, bf16[448,512]{1,0:T(8,128)(2,1)} %bitcast.9, bf16[32,16,2048]{2,1,0:T(8,128)(2,1)} %copy-done, bf16[32,16,768]{2,1,0:T(8,128)(2,1)} %copy-done.1), custom_call_target="tpu_custom_call" | custom-call | flops 704643072 | bytes 4194304 | tf_op jit(solution)/shard_map/whole/pallas_call | solution.py:121
  98.2 9.7 %collective-permute-done.1.x_ref = bf16[32,16,1280]{2,1,0:T(8,128)(2,1)} collective-permute-done((bf16[32,16,1280]{2,1,0:T(8,128)(2,1)}, bf16[32,16,1280]{2,1,0:T(8,128)(2,1)}, u32[]{:S(2)}, u32[]{:S(2)}) %collective-permute-start.1) | collective-permute-done | bytes 1310752 | tf_op jit(solution)/shard_map/ppermute | solution.py:290
  107.9 5.5 %rest.1 = (bf16[448,2048]{1,0:T(8,128)(2,1)}, f32[8,256]{1,0:T(8,128)}) custom-call(bf16[448,512]{1,0:T(8,128)(2,1)} %bitcast.10, bf16[32,16,1280]{2,1,0:T(8,128)(2,1)} %collective-permute-done.1.x_ref, f32[448,1280]{1,0:T(8,128)} %partial.1.p_ref, f32[448,224]{1,0:T(8,128)} %get-tuple-element.12.g_ref, ...), custom_call_target="tpu_custom_call", output_to_operand_aliasing={{0}: (4, {})} | custom-call | flops 587202560 | bytes 4194304 | tf_op jit(solution)/shard_map/rest/pallas_call | solution.py:194
  113.3 0.7 broadcast_in_dim.13
  114.0 13.4 %all_to_all.25 = f32[16,8,256]{2,1,0:T(8,128)S(1)} all-to-all(f32[16,8,256]{2,1,0:T(8,128)S(1)} %broadcast_in_dim.13), channel_id=1, replica_groups=mesh['y'=4,'zh'=2,'x'=4,'c'=2,'zl'=4] {'y','x'}, dimensions={0} | all-to-all | bytes 262144 | tf_op jit(solution)/shard_map/all_to_all | solution.py:270
  127.5 46.7 %all_to_all.26.t_ref = f32[16,8,256]{2,1,0:T(8,128)} all-to-all(f32[16,8,256]{2,1,0:T(8,128)S(1)} %broadcast_in_dim.14), channel_id=1, replica_groups=mesh['y'=4,'zh'=2,'x'=4,'c'=2,'zl'=4] {'zh','zl','c'}, dimensions={0} | all-to-all | bytes 262144 | tf_op jit(solution)/shard_map/all_to_all | solution.py:270
  174.2 5.5 %power.1 = f32[448,2048]{1,0:T(8,128)} custom-call(f32[16,8,256]{2,1,0:T(8,128)} %all_to_all.26.t_ref, bf16[448,2048]{1,0:T(8,128)(2,1)} %get-tuple-element.14.s_ref), custom_call_target="tpu_custom_call" | custom-call | tf_op jit(solution)/shard_map/power/pallas_call | solution.py:253
  (6 shorter events, 0.0 us)
Async XLA Ops:
  3.3 28.0 %all-to-all-start = ((bf16[32,16,1280]{2,1,0:T(8,128)(2,1)}), bf16[32,16,1280]{2,1,0:T(8,128)(2,1)}, u32[]{:S(2)}, u32[]{:S(2)}) async-start(bf16[32,16,1280]{2,1,0:T(8,128)(2,1)} %pack.4), calls=%async_computation | async-start | bytes 2621440 | tf_op jit(solution)/shard_map/all_to_all | solution.py:274
  31.3 36.5 %all-to-all-start.1 = ((bf16[32,16,2048]{2,1,0:T(8,128)(2,1)}), bf16[32,16,2048]{2,1,0:T(8,128)(2,1)S(1)}, u32[]{:S(2)}, u32[]{:S(2)}) async-start(bf16[32,16,2048]{2,1,0:T(8,128)(2,1)} %pack.5), calls=%async_computation.1 | async-start | bytes 4194304 | tf_op jit(solution)/shard_map/all_to_all | solution.py:274
  36.4 9.3 %copy-start.3 = (s32[7]{0:T(128)S(1)}, s32[7]{0:T(128)}, u32[]{:S(2)}) copy-start(s32[7]{0:T(128)} %param.4) | copy-start | bytes 88
  36.4 9.7 %copy-start.4 = (s32[32]{0:T(128)S(1)}, s32[32]{0:T(128)}, u32[]{:S(2)}) copy-start(s32[32]{0:T(128)} %param.5) | copy-start | bytes 388
  38.7 28.1 %collective-permute-start = (bf16[32,16,768]{2,1,0:T(8,128)(2,1)}, bf16[32,16,768]{2,1,0:T(8,128)(2,1)S(1)}, u32[]{:S(2)}, u32[]{:S(2)}) collective-permute-start(bf16[32,16,768]{2,1,0:T(8,128)(2,1)} %pack.3), channel_id=1, source_target_pairs={{0,32},{32,0},{1,33},{33,1},{2,34},{34,2},{3,35},{35,3},{4,36},{36... | collective-permute-start | bytes 2359304 | tf_op jit(solution)/shard_map/ppermute | solution.py:287
  46.0 61.8 %collective-permute-start.1 = (bf16[32,16,1280]{2,1,0:T(8,128)(2,1)}, bf16[32,16,1280]{2,1,0:T(8,128)(2,1)}, u32[]{:S(2)}, u32[]{:S(2)}) collective-permute-start(bf16[32,16,1280]{2,1,0:T(8,128)(2,1)} %all-to-all-done), channel_id=1, source_target_pairs={{0,32},{32,0},{1,33},{33,1},{2,34},{34,2},{3,35},{35,3},{4,36},{36... | collective-permute-start | bytes 3932168 | tf_op jit(solution)/shard_map/ppermute | solution.py:290
  66.9 0.9 copy-start.2
  67.7 10.0 %copy-start = (bf16[32,16,2048]{2,1,0:T(8,128)(2,1)}, bf16[32,16,2048]{2,1,0:T(8,128)(2,1)S(1)}, u32[]{:S(2)}) copy-start(bf16[32,16,2048]{2,1,0:T(8,128)(2,1)S(1)} %all-to-all-done.1.x_ref.x0_ref) | copy-start | bytes 6291460
  67.7 24.4 %all-to-all-start.2 = ((bf16[32,16,768]{2,1,0:T(8,128)(2,1)}), bf16[32,16,768]{2,1,0:T(8,128)(2,1)S(1)}, u32[]{:S(2)}, u32[]{:S(2)}) async-start(bf16[32,16,768]{2,1,0:T(8,128)(2,1)} %copy-done.2), calls=%async_computation.2 | async-start | bytes 1572864 | tf_op jit(solution)/shard_map/all_to_all | solution.py:274
  92.1 0.9 copy-start.1

commit v3 on v2

--- a/solution.py
+++ b/solution.py
@@ -92,7 +92,7 @@
 
 def gram_of(parts):
     real, imag = parts[:HALF], parts[HALF:]
-    return dot_t(parts, real) + dot_t(jnp.concatenate([imag, -real], axis=0), imag)
+    return jnp.concatenate([dot_t(real, real) + dot_t(imag, imag), dot_t(imag, real)], axis=0)
 
 
 def rows_of(ref):
@@ -160,57 +160,6 @@
     return lax.broadcasted_iota(jnp.int32, (rows, HALF), 1) // NF
 
 
-def rest_kernel(steps, w_ref, x_ref, p_ref, g_ref, _, s_ref, t_ref, acc):
-    step = pl.program_id(0)
-    parts = (p_ref[...] + dot(w_ref[...], rows_of(x_ref))).astype(BF16)
-    emit(parts, s_ref)
-    gram = gram_of(parts)
-
-    @pl.when(step == 0)
-    def _():
-        acc[...] = g_ref[...] + gram
-
-    @pl.when(step > 0)
-    def _():
-        acc[...] += gram
-
-    @pl.when(step == steps - 1)
-    def _():
-        kept = jnp.where(same_freq(ROWS), acc[...], 0.0)
-        tables = kept.reshape(2 * NB, NF, HALF).sum(axis=1)
-        block = lax.broadcasted_iota(jnp.int32, (NB, HALF), 0)
-        t_ref[...] = jnp.zeros_like(t_ref)
-        for k in range(PAIRS + 1):
-            pick = (lane_block(NB) + k) % NB == block
-            t_ref[k : k + 1, :HALF] = jnp.where(pick, tables[:NB], 0.0).sum(axis=0, keepdims=True)
-            if k:
-                row = PAIRS + k
-                t_ref[row : row + 1, :HALF] = jnp.where(pick, tables[NB:], 0.0).sum(axis=0, keepdims=True)
-
-
-def rest(w, x, p, g, s, width):
-    times = w.shape[1]
-    steps = x.shape[2] // width
-    return pl.pallas_call(
-        functools.partial(rest_kernel, steps),
-        grid=(steps,),
-        out_shape=(jax.ShapeDtypeStruct(s.shape, BF16), jax.ShapeDtypeStruct((8, 256), F32)),
-        in_specs=[
-            pl.BlockSpec((ROWS, times), lambda i: (0, 0)),
-            pl.BlockSpec((*x.shape[:2], width), lambda i: (0, 0, i)),
-            pl.BlockSpec((ROWS, width), lambda i: (0, i)),
-            pl.BlockSpec((ROWS, HALF), lambda i: (0, 0)),
-            pl.BlockSpec(memory_space=pl.ANY),
-        ],
-        out_specs=(pl.BlockSpec((ROWS, width), lambda i: (0, i)), pl.BlockSpec((8, 256), lambda i: (0, 0))),
-        scratch_shapes=[pltpu.VMEM((ROWS, HALF), F32)],
-        input_output_aliases={4: 0},
-        compiler_params=PARAMS,
-        cost_estimate=pl.CostEstimate(flops=2 * ROWS * times * x.shape[2], bytes_accessed=2**22, transcendentals=0),
-        name="rest",
-    )(w, x, p, g, s)
-
-
 def turned(row, k):
     lane = lax.broadcasted_iota(jnp.int32, row.shape, 1)
     near = pltpu.roll(row, 256 - k * NF, 1)
@@ -218,49 +167,107 @@
     return jnp.where(lane < HALF - k * NF, near, far)
 
 
-def power_kernel(denominator, t_ref, s_ref, o_ref, m_ref):
-    @pl.when(pl.program_id(0) == 0)
-    def _():
-        sums = jnp.sum(t_ref[...], axis=0) / denominator
-        real_rows = [sums[k : k + 1, :] for k in range(PAIRS + 1)]
-        imag_rows = [jnp.zeros_like(real_rows[0])] + [sums[PAIRS + k : PAIRS + k + 1, :] for k in range(1, PAIRS + 1)]
-        for k in range(PAIRS + 1, NB):
-            real_rows.append(turned(real_rows[NB - k], k))
-            imag_rows.append(-turned(imag_rows[NB - k], k))
-        same = same_freq(NF)
-        block = lane_block(1)
-        for b in range(NB):
-            re = sum(jnp.where((block + k) % NB == b, real_rows[k][:, :HALF], 0.0) for k in range(NB))
-            im = sum(jnp.where((block + k) % NB == b, imag_rows[k][:, :HALF], 0.0) for k in range(NB))
-            re = jnp.where(same, jnp.broadcast_to(re, (NF, HALF)), 0.0)
-            im = jnp.where(same, jnp.broadcast_to(im, (NF, HALF)), 0.0)
-            at = b * 2 * NF
-            for part, (on_real, on_imag) in enumerate(((re, -im), (im, re))):
-                for side, value in enumerate((on_real, on_imag)):
-                    high = value.astype(BF16)
-                    rows = slice(at + part * NF, at + (part + 1) * NF)
-                    m_ref[2 * side, rows, :] = high
-                    m_ref[2 * side + 1, rows, :] = (value - high.astype(F32)).astype(BF16)
-
-    real = jnp.concatenate([s_ref[b * 2 * NF : b * 2 * NF + NF, :] for b in range(NB)], axis=0)
-    imag = jnp.concatenate([s_ref[b * 2 * NF + NF : (b + 1) * 2 * NF, :] for b in range(NB)], axis=0)
-    low = dot(m_ref[1], real) + dot(m_ref[3], imag)
-    o_ref[...] = low + dot(m_ref[0], real) + dot(m_ref[2], imag)
+def rest_kernel(w_ref, x_ref, p_ref, g_ref, _, s_ref, t_ref, part_ref, row_ref, sem):
+    width = x_ref.shape[2]
+    parts = (p_ref[...] + dot(w_ref[...], rows_of(x_ref))).astype(BF16)
+    emit(parts, part_ref)
+    save = pltpu.make_async_copy(part_ref, s_ref.at[:, pl.ds(0, width)], sem)
+    save.start()
+    kept = jnp.where(same_freq(ROWS), g_ref[...] + gram_of(parts), 0.0)
+    tables = kept.reshape(2 * NB, NF, HALF).sum(axis=1)
+    block = lax.broadcasted_iota(jnp.int32, (NB, HALF), 0)
+    row_ref[...] = jnp.zeros_like(row_ref)
+    for k in range(NB):
+        pick = (lane_block(NB) + k) % NB == block
+        if k <= PAIRS:
+            row_ref[k : k + 1, :HALF] = jnp.where(pick, tables[:NB], 0.0).sum(axis=0, keepdims=True)
+        if k:
+            row_ref[NB + k : NB + k + 1, :HALF] = jnp.where(pick, tables[NB:], 0.0).sum(axis=0, keepdims=True)
+    rows = [row_ref[k : k + 1, :] for k in range(2 * NB)]
+    imag = [rows[NB + k] - turned(rows[2 * NB - k], k) for k in range(1, PAIRS + 1)]
+    sums = jnp.concatenate(rows[: PAIRS + 1] + imag + [jnp.zeros_like(imag[0])], axis=0)
+    for i in range(t_ref.shape[0]):
+        t_ref[i] = sums
+    save.wait()
+
+
+def rest(w, x, p, g, s, copies):
+    times = w.shape[1]
+    width = x.shape[2]
+    here = pl.BlockSpec(memory_space=pltpu.VMEM)
+    there = pl.BlockSpec(memory_space=pl.ANY)
+    return pl.pallas_call(
+        rest_kernel,
+        out_shape=(jax.ShapeDtypeStruct(s.shape, BF16), jax.ShapeDtypeStruct((copies, 8, 256), F32)),
+        in_specs=[here, here, here, here, there],
+        out_specs=(there, here),
+        scratch_shapes=[pltpu.VMEM((ROWS, width), BF16), pltpu.VMEM((16, 256), F32), pltpu.SemaphoreType.DMA],
+        input_output_aliases={4: 0},
+        compiler_params=pltpu.CompilerParams(vmem_limit_bytes=16 * 2**20),
+        cost_estimate=pl.CostEstimate(flops=2 * ROWS * times * width, bytes_accessed=2**22, transcendentals=0),
+        name="rest",
+    )(w, x, p, g, s)
+
+
+def spread_to(part):
+    row = lax.broadcasted_iota(jnp.int32, (HALF, ROWS), 0)
+    col = lax.broadcasted_iota(jnp.int32, (HALF, ROWS), 1)
+    return (col == row // NF * 2 * NF + part * NF + row % NF).astype(BF16)
+
+
+def power_kernel(denominator, t_ref, s_ref, o_ref, m_ref, in_ref, out_ref, in_sem, out_sem):
+    steps, _, width = in_ref.shape
+    loads = []
+    for i in range(steps):
+        loads.append(pltpu.make_async_copy(s_ref.at[:, pl.ds(i * width, width)], in_ref.at[i], in_sem.at[i]))
+        loads[i].start()
+    sums = jnp.sum(t_ref[...], axis=0) / denominator
+    real_rows = [sums[k : k + 1, :] for k in range(PAIRS + 1)]
+    imag_rows = [jnp.zeros_like(real_rows[0])] + [sums[PAIRS + k : PAIRS + k + 1, :] for k in range(1, PAIRS + 1)]
+    for k in range(PAIRS + 1, NB):
+        real_rows.append(turned(real_rows[NB - k], k))
+        imag_rows.append(-turned(imag_rows[NB - k], k))
+    block = lane_block(1)
+    tables = []
+    for rows in (real_rows, imag_rows):
+        picked = [sum(jnp.where((block + k) % NB == b, rows[k][:, :HALF], 0.0) for k in range(NB)) for b in range(NB)]
+        tables.append(jnp.concatenate(picked, axis=0).astype(BF16))
+    real, imag = tables
+    spread = [spread_to(part) for part in range(2)]
+    from_real = dot(real, spread[0]) - dot(imag, spread[1])
+    from_imag = dot(imag, spread[0]) + dot(real, spread[1])
+    same = lax.broadcasted_iota(jnp.int32, (NF, ROWS), 0) == lax.broadcasted_iota(jnp.int32, (NF, ROWS), 1) % NF
+    for b in range(NB):
+        for part, table in enumerate((from_real, from_imag)):
+            at = (2 * b + part) * NF
+            row = jnp.broadcast_to(table[b : b + 1], (NF, ROWS))
+            m_ref[at : at + NF, :] = jnp.where(same, row, 0.0).astype(BF16)
+    stores = []
+    for i in range(steps):
+        loads[i].wait()
+        out_ref[i] = dot(m_ref[...], in_ref[i])
+        stores.append(pltpu.make_async_copy(out_ref.at[i], o_ref.at[:, pl.ds(i * width, width)], out_sem.at[i]))
+        stores[i].start()
+    for store in stores:
+        store.wait()
 
 
 def power(t, s, denominator):
     pts = s.shape[1]
+    steps = pts // WIDTH
     return pl.pallas_call(
         functools.partial(power_kernel, denominator),
-        grid=(pts // WIDTH,),
         out_shape=jax.ShapeDtypeStruct((ROWS, pts), F32),
-        in_specs=[
-            pl.BlockSpec(t.shape, lambda i: (0, 0, 0)),
-            pl.BlockSpec((ROWS, WIDTH), lambda i: (0, i)),
+        in_specs=[pl.BlockSpec(memory_space=pltpu.VMEM), pl.BlockSpec(memory_space=pl.ANY)],
+        out_specs=pl.BlockSpec(memory_space=pl.ANY),
+        scratch_shapes=[
+            pltpu.VMEM((ROWS, ROWS), BF16),
+            pltpu.VMEM((steps, ROWS, WIDTH), BF16),
+            pltpu.VMEM((steps, ROWS, WIDTH), F32),
+            pltpu.SemaphoreType.DMA((steps,)),
+            pltpu.SemaphoreType.DMA((steps,)),
         ],
-        out_specs=pl.BlockSpec((ROWS, WIDTH), lambda i: (0, i)),
-        scratch_shapes=[pltpu.VMEM((4, ROWS, HALF), BF16)],
-        compiler_params=PARAMS,
+        compiler_params=pltpu.CompilerParams(vmem_limit_bytes=65_300_000),
         name="power",
     )(t, s)
 
@@ -299,8 +306,8 @@
     first = exchange(first, PLANE)
     p = partial(w0, x0, later, 640)
     s, g = whole(w0, w1, x0, first, 256)
-    s, t = rest(w1, passed, p, g, s, 640)
-    t = to_all(t, ("y", "x")).sum(axis=0)
+    s, t = rest(w1, passed, p, g, s, lax.axis_size(("y", "x")))
+    t = exchange(t, ("y", "x")).sum(axis=0)
     t = to_all(t, ("zh", "zl", "c"))
     out = power(t, s, float(NB * total))
     shape = (1, NB, 2, NF, own)

time: 181 us -> 178 us (0.983)
  Pallas kernels: 27.5 us -> 24.5 us
    all_to_all x2 -> x1, blocking collectives: 60.1 us -> 46.7 us  [to_all(): return lax.all_to_all(copies, axes, 0, 0, tiled=True)]
    all_to_all x0 -> x1, blocking collectives: none -> 13.4 us  [exchange(): return lax.all_to_all(x, axes, 0, 0, tiled=True)]
    pallas_call x2, Pallas kernels: 11 us -> 8.07 us  [the longest x1 4.52 us: power(): pl.pallas_call(functools.partial(power_kernel, denominator), out_shape=ja...]
where the time goes in v3:
time: 178 us; the launch traced here: 177 us
  blocking collectives  60.1 us (34%)
  waiting for transfers between devices  52.2 us (29%)
  starting transfers between devices  30.9 us (17%)
  Pallas kernels  24.5 us (14%)
  other arithmetic  5.88 us (3%)
  local copies, waits for them, and re-layouts  2.84 us (2%)
    all_to_all x1, blocking collectives, to_all(): return lax.all_to_all(copies, axes, 0, 0, tiled=True)  46.7 us
    all_to_all x3, waiting for transfers between devices, exchange(): return lax.all_to_all(x, axes, 0, 0, tiled=True)  27.2 us
    all_to_all x3, starting transfers between devices, exchange(): return lax.all_to_all(x, axes, 0, 0, tiled=True)  23.8 us
    ppermute x1, waiting for transfers between devices, shards(): first = lax.ppermute(first, 'zh', swap)  15.1 us
    all_to_all x1, blocking collectives, exchange(): return lax.all_to_all(x, axes, 0, 0, tiled=True)  13.4 us
    ppermute x1, waiting for transfers between devices, shards(): passed = lax.ppermute(pass_on, 'zh', swap)  9.86 us
    pallas_call x3, Pallas kernels, pack(): pl.pallas_call(functools.partial(pack_kernel, own, [job[:2] for job in jo...  8.1 us
    ppermute x1, starting transfers between devices, shards(): first = lax.ppermute(first, 'zh', swap)  7 us
  transfers between devices with their start and end apart: 5, of which 4 were waited for; matrix products, arithmetic and copies ran while one was open for 3% of the time, Pallas kernels for 8%

profile of v3, /device:TPU:1, one launch (start us, length us, event | category | flops | bytes accessed | tf_op | source)
XLA Modules:
  0.0 177.1 jit_solution(12334166593045635496)
XLA Ops:
  0.6 2.6 %pack.4 = bf16[32,16,1280]{2,1,0:T(8,128)(2,1)} custom-call(bf16[16,131072]{1,0:T(8,128)(2,1)} %bitcast.7), custom_call_target="tpu_custom_call" | custom-call | tf_op jit(solution)/shard_map/pack/pallas_call | solution.py:75
  3.3 8.6 %all-to-all-start = ((bf16[32,16,1280]{2,1,0:T(8,128)(2,1)}), bf16[32,16,1280]{2,1,0:T(8,128)(2,1)}, u32[]{:S(2)}, u32[]{:S(2)}) async-start(bf16[32,16,1280]{2,1,0:T(8,128)(2,1)} %pack.4), calls=%async_computation | async-start | bytes 2621440 | tf_op jit(solution)/shard_map/all_to_all | solution.py:281
  11.9 3.2 %pack.5 = bf16[32,16,2048]{2,1,0:T(8,128)(2,1)} custom-call(bf16[16,131072]{1,0:T(8,128)(2,1)} %bitcast.8), custom_call_target="tpu_custom_call" | custom-call | tf_op jit(solution)/shard_map/pack/pallas_call | solution.py:75
  15.1 16.1 %all-to-all-done = bf16[32,16,1280]{2,1,0:T(8,128)(2,1)} async-done(((bf16[32,16,1280]{2,1,0:T(8,128)(2,1)}), bf16[32,16,1280]{2,1,0:T(8,128)(2,1)}, u32[]{:S(2)}, u32[]{:S(2)}) %all-to-all-start) | async-done | bytes 1310752 | tf_op jit(solution)/shard_map/all_to_all | solution.py:281
  31.3 5.2 %all-to-all-start.1 = ((bf16[32,16,2048]{2,1,0:T(8,128)(2,1)}), bf16[32,16,2048]{2,1,0:T(8,128)(2,1)S(1)}, u32[]{:S(2)}, u32[]{:S(2)}) async-start(bf16[32,16,2048]{2,1,0:T(8,128)(2,1)} %pack.5), calls=%async_computation.1 | async-start | bytes 4194304 | tf_op jit(solution)/shard_map/all_to_all | solution.py:281
  36.4 0.0 copy-start.6
  36.4 0.0 copy-start.7
  36.5 2.3 %pack.3 = bf16[32,16,768]{2,1,0:T(8,128)(2,1)} custom-call(bf16[16,131072]{1,0:T(8,128)(2,1)} %bitcast.9), custom_call_target="tpu_custom_call" | custom-call | tf_op jit(solution)/shard_map/pack/pallas_call | solution.py:75
  38.7 7.0 %collective-permute-start = (bf16[32,16,768]{2,1,0:T(8,128)(2,1)}, bf16[32,16,768]{2,1,0:T(8,128)(2,1)S(1)}, u32[]{:S(2)}, u32[]{:S(2)}) collective-permute-start(bf16[32,16,768]{2,1,0:T(8,128)(2,1)} %pack.3), channel_id=1, source_target_pairs={{0,32},{32,0},{1,33},{33,1},{2,34},{34,2},{3,35},{35,3},{4,36},{36... | collective-permute-start | bytes 2359304 | tf_op jit(solution)/shard_map/ppermute | solution.py:294
  45.7 0.0 copy-done.6
  45.7 0.1 subtract_select_fusion
  45.8 0.2 fusion.15
  46.0 0.1 collective-permute-start.1
  46.1 3.9 %multiply_convert_fusion.1 = (bf16[1,7,32,512]{3,2,1,0:T(8,128)(2,1)S(1)}, bf16[1,7,32,512]{3,2,1,0:T(8,128)(2,1)S(1)}, bf16[1,7,32,512]{3,2,1,0:T(8,128)(2,1)S(1)}, bf16[1,7,32,512]{3,2,1,0:T(8,128)(2,1)S(1)}) fusion(f32[7,512]{1,0:T(8,128)S(1)} %get-tuple-element.20, s32[7,512]{1,0:T(8,128)S(1)} %get-tuple-element.28, s32[32]{0:T(128)S(1)} %copy-done.7, ...), kind=kLoop, calls=%fused_computation.19 | loop fusion | flops 4587520 | bytes 1003648 | tf_op jit(solution)/shard_map/convert
  50.1 0.8 pad_maximum_fusion.1
  50.9 0.8 pad_maximum_fusion
  51.7 15.1 %collective-permute-done = bf16[32,16,768]{2,1,0:T(8,128)(2,1)S(1)} collective-permute-done((bf16[32,16,768]{2,1,0:T(8,128)(2,1)}, bf16[32,16,768]{2,1,0:T(8,128)(2,1)S(1)}, u32[]{:S(2)}, u32[]{:S(2)}) %collective-permute-start) | collective-permute-done | bytes 786464 | tf_op jit(solution)/shard_map/ppermute | solution.py:294
  66.9 0.9 copy-done.5
  67.7 0.0 all-to-all-done.1.x_ref.x0_ref
  67.7 10.0 %all-to-all-start.2 = ((bf16[32,16,768]{2,1,0:T(8,128)(2,1)}), bf16[32,16,768]{2,1,0:T(8,128)(2,1)S(1)}, u32[]{:S(2)}, u32[]{:S(2)}) async-start(bf16[32,16,768]{2,1,0:T(8,128)(2,1)} %copy-done.5), calls=%async_computation.2 | async-start | bytes 1572864 | tf_op jit(solution)/shard_map/all_to_all | solution.py:281
  77.8 0.0 copy-done.3
  77.8 3.3 %partial.1.p_ref = f32[448,1280]{1,0:T(8,128)} custom-call(bf16[448,512]{1,0:T(8,128)(2,1)} %bitcast.11, bf16[32,16,2048]{2,1,0:T(8,128)(2,1)} %copy-done.3), custom_call_target="tpu_custom_call" | custom-call | flops 587202560 | bytes 2097152 | tf_op jit(solution)/shard_map/partial/pallas_call | solution.py:144
  81.1 11.1 %all-to-all-done.2.x1_ref = bf16[32,16,768]{2,1,0:T(8,128)(2,1)S(1)} async-done(((bf16[32,16,768]{2,1,0:T(8,128)(2,1)}), bf16[32,16,768]{2,1,0:T(8,128)(2,1)S(1)}, u32[]{:S(2)}, u32[]{:S(2)}) %all-to-all-start.2) | async-done | bytes 786464 | tf_op jit(solution)/shard_map/all_to_all | solution.py:281
  92.1 0.9 copy-done.4
  93.0 5.0 %whole.1 = (bf16[448,2048]{1,0:T(8,128)(2,1)}, f32[448,224]{1,0:T(8,128)}) custom-call(bf16[448,512]{1,0:T(8,128)(2,1)} %bitcast.12, bf16[448,512]{1,0:T(8,128)(2,1)} %bitcast.5, bf16[32,16,2048]{2,1,0:T(8,128)(2,1)} %copy-done.3, bf16[32,16,768]{2,1,0:T(8,128)(2,1)} %copy-done.4), custom_call_target="tpu_custom_call" | custom-call | flops 704643072 | bytes 4194304 | tf_op jit(solution)/shard_map/whole/pallas_call | solution.py:121
  98.0 9.9 %collective-permute-done.1.x_ref = bf16[32,16,1280]{2,1,0:T(8,128)(2,1)} collective-permute-done((bf16[32,16,1280]{2,1,0:T(8,128)(2,1)}, bf16[32,16,1280]{2,1,0:T(8,128)(2,1)}, u32[]{:S(2)}, u32[]{:S(2)}) %collective-permute-start.1) | collective-permute-done | bytes 1310752 | tf_op jit(solution)/shard_map/ppermute | solution.py:297
  107.9 0.0 copy-done
  107.9 1.0 copy-done.2
  108.9 3.6 %rest.1 = (bf16[448,2048]{1,0:T(8,128)(2,1)}, f32[16,8,256]{2,1,0:T(8,128)S(1)}) custom-call(bf16[448,512]{1,0:T(8,128)(2,1)S(1)} %bitcast.6, bf16[32,16,1280]{2,1,0:T(8,128)(2,1)} %collective-permute-done.1.x_ref, f32[448,1280]{1,0:T(8,128)S(1)} %copy-done, f32[448,224]{1,0:T(8,128)S(1)} %copy-done.2, ...), custom_call_target="tpu_custom_call", output_to_operand_aliasing={{0}: (4, {})} | custom-call | flops 587202560 | bytes 4194304 | tf_op jit(solution)/shard_map/rest/pallas_call | solution.py:199
  112.5 13.4 %all_to_all.25 = f32[16,8,256]{2,1,0:T(8,128)S(1)} all-to-all(f32[16,8,256]{2,1,0:T(8,128)S(1)} %get-tuple-element.15), channel_id=1, replica_groups=mesh['y'=4,'zh'=2,'x'=4,'c'=2,'zl'=4] {'y','x'}, dimensions={0} | all-to-all | bytes 262144 | tf_op jit(solution)/shard_map/all_to_all | solution.py:281
  125.9 46.7 %all_to_all.26.t_ref = f32[16,8,256]{2,1,0:T(8,128)} all-to-all(f32[16,8,256]{2,1,0:T(8,128)S(1)} %broadcast_in_dim.11), channel_id=1, replica_groups=mesh['y'=4,'zh'=2,'x'=4,'c'=2,'zl'=4] {'zh','zl','c'}, dimensions={0} | all-to-all | bytes 262144 | tf_op jit(solution)/shard_map/all_to_all | solution.py:277
  172.6 4.5 %power.1 = f32[448,2048]{1,0:T(8,128)} custom-call(f32[16,8,256]{2,1,0:T(8,128)} %all_to_all.26.t_ref, bf16[448,2048]{1,0:T(8,128)(2,1)} %get-tuple-element.14.s_ref), custom_call_target="tpu_custom_call" | custom-call | tf_op jit(solution)/shard_map/power/pallas_call | solution.py:258
  (11 shorter events, 0.0 us)
Async XLA Ops:
  3.3 28.0 %all-to-all-start = ((bf16[32,16,1280]{2,1,0:T(8,128)(2,1)}), bf16[32,16,1280]{2,1,0:T(8,128)(2,1)}, u32[]{:S(2)}, u32[]{:S(2)}) async-start(bf16[32,16,1280]{2,1,0:T(8,128)(2,1)} %pack.4), calls=%async_computation | async-start | bytes 2621440 | tf_op jit(solution)/shard_map/all_to_all | solution.py:281
  31.3 36.5 %all-to-all-start.1 = ((bf16[32,16,2048]{2,1,0:T(8,128)(2,1)}), bf16[32,16,2048]{2,1,0:T(8,128)(2,1)S(1)}, u32[]{:S(2)}, u32[]{:S(2)}) async-start(bf16[32,16,2048]{2,1,0:T(8,128)(2,1)} %pack.5), calls=%async_computation.1 | async-start | bytes 4194304 | tf_op jit(solution)/shard_map/all_to_all | solution.py:281
  36.4 9.3 %copy-start.6 = (s32[7]{0:T(128)S(1)}, s32[7]{0:T(128)}, u32[]{:S(2)}) copy-start(s32[7]{0:T(128)} %param.4) | copy-start | bytes 88
  36.4 9.7 %copy-start.7 = (s32[32]{0:T(128)S(1)}, s32[32]{0:T(128)}, u32[]{:S(2)}) copy-start(s32[32]{0:T(128)} %param.5) | copy-start | bytes 388
  38.7 28.1 %collective-permute-start = (bf16[32,16,768]{2,1,0:T(8,128)(2,1)}, bf16[32,16,768]{2,1,0:T(8,128)(2,1)S(1)}, u32[]{:S(2)}, u32[]{:S(2)}) collective-permute-start(bf16[32,16,768]{2,1,0:T(8,128)(2,1)} %pack.3), channel_id=1, source_target_pairs={{0,32},{32,0},{1,33},{33,1},{2,34},{34,2},{3,35},{35,3},{4,36},{36... | collective-permute-start | bytes 2359304 | tf_op jit(solution)/shard_map/ppermute | solution.py:294
  46.0 61.8 %collective-permute-start.1 = (bf16[32,16,1280]{2,1,0:T(8,128)(2,1)}, bf16[32,16,1280]{2,1,0:T(8,128)(2,1)}, u32[]{:S(2)}, u32[]{:S(2)}) collective-permute-start(bf16[32,16,1280]{2,1,0:T(8,128)(2,1)} %all-to-all-done), channel_id=1, source_target_pairs={{0,32},{32,0},{1,33},{33,1},{2,34},{34,2},{3,35},{35,3},{4,36},{36... | collective-permute-start | bytes 3932168 | tf_op jit(solution)/shard_map/ppermute | solution.py:297
  66.9 0.9 copy-start.5
  67.7 10.0 %copy-start.3 = (bf16[32,16,2048]{2,1,0:T(8,128)(2,1)}, bf16[32,16,2048]{2,1,0:T(8,128)(2,1)S(1)}, u32[]{:S(2)}) copy-start(bf16[32,16,2048]{2,1,0:T(8,128)(2,1)S(1)} %all-to-all-done.1.x_ref.x0_ref) | copy-start | bytes 6291460
  67.7 24.4 %all-to-all-start.2 = ((bf16[32,16,768]{2,1,0:T(8,128)(2,1)}), bf16[32,16,768]{2,1,0:T(8,128)(2,1)S(1)}, u32[]{:S(2)}, u32[]{:S(2)}) async-start(bf16[32,16,768]{2,1,0:T(8,128)(2,1)} %copy-done.5), calls=%async_computation.2 | async-start | bytes 1572864 | tf_op jit(solution)/shard_map/all_to_all | solution.py:281
  81.1 26.8 %copy-start = (f32[448,1280]{1,0:T(8,128)S(1)}, f32[448,1280]{1,0:T(8,128)}, u32[]{:S(2)}) copy-start(f32[448,1280]{1,0:T(8,128)} %partial.1.p_ref) | copy-start | bytes 6881284
  81.1 26.8 %copy-start.1 = (bf16[2,7,32,512]{3,2,1,0:T(8,128)(2,1)S(1)}, bf16[2,7,32,512]{3,2,1,0:T(8,128)(2,1)}, u32[]{:S(2)}) copy-start(bf16[2,7,32,512]{3,2,1,0:T(8,128)(2,1)} %pad_maximum_fusion.1) | copy-start | bytes 1376260
  92.1 0.9 copy-start.4
  107.9 1.0 copy-start.2

commit v4 on v3

--- a/solution.py
+++ b/solution.py
@@ -19,9 +19,10 @@
 TA = ("y", "zh", "x", "c")
 PLANE = ("y", "x", "c")
 FIRST = 768
-WIDTH = 512
+LAST = 512
 F32 = jnp.float32
 BF16 = jnp.bfloat16
+SMALL = pltpu.CompilerParams(dimension_semantics=("arbitrary",), vmem_limit_bytes=16 * 2**20)
 PARAMS = pltpu.CompilerParams(dimension_semantics=("arbitrary",), vmem_limit_bytes=60 * 2**20)
 
 
@@ -99,9 +100,10 @@
     return ref[...].reshape(-1, ref.shape[2])
 
 
-def whole_kernel(w0_ref, w1_ref, x0_ref, x1_ref, s_ref, g_ref):
+def whole_kernel(w0_ref, w1_ref, x0_ref, x1_ref, s_ref, g_ref, part_ref):
     parts = (dot(w0_ref[...], rows_of(x0_ref)) + dot(w1_ref[...], rows_of(x1_ref))).astype(BF16)
     emit(parts, s_ref)
+    emit(parts, part_ref)
     gram = gram_of(parts)
 
     @pl.when(pl.program_id(0) == 0)
@@ -121,15 +123,23 @@
     return pl.pallas_call(
         whole_kernel,
         grid=(count // width,),
-        out_shape=(jax.ShapeDtypeStruct((ROWS, pts), BF16), jax.ShapeDtypeStruct((ROWS, HALF), F32)),
+        out_shape=(
+            jax.ShapeDtypeStruct((ROWS, pts), BF16),
+            jax.ShapeDtypeStruct((ROWS, HALF), F32),
+            jax.ShapeDtypeStruct((ROWS, count), BF16),
+        ),
         in_specs=[
             fixed,
             fixed,
             pl.BlockSpec((*x0.shape[:2], width), lambda i: (0, 0, i + skip)),
             pl.BlockSpec((*x0.shape[:2], width), lambda i: (0, 0, i)),
         ],
-        out_specs=(pl.BlockSpec((ROWS, width), lambda i: (0, i + skip)), pl.BlockSpec((ROWS, HALF), lambda i: (0, 0))),
-        compiler_params=PARAMS,
+        out_specs=(
+            pl.BlockSpec((ROWS, width), lambda i: (0, i + skip)),
+            pl.BlockSpec((ROWS, HALF), lambda i: (0, 0)),
+            pl.BlockSpec((ROWS, width), lambda i: (0, i)),
+        ),
+        compiler_params=SMALL,
         cost_estimate=pl.CostEstimate(flops=4 * ROWS * times * count, bytes_accessed=2**22, transcendentals=0),
         name="whole",
     )(w0, w1, x0, x1)
@@ -139,15 +149,16 @@
     p_ref[...] = dot(w_ref[...], rows_of(x_ref))
 
 
-def partial(w, x, pts, width):
+def partial(w, x, low, pts, width):
     times = w.shape[1]
+    skip = low // width
     return pl.pallas_call(
         partial_kernel,
         grid=(pts // width,),
         out_shape=jax.ShapeDtypeStruct((ROWS, pts), F32),
         in_specs=[
             pl.BlockSpec((ROWS, times), lambda i: (0, 0)),
-            pl.BlockSpec((*x.shape[:2], width), lambda i: (0, 0, i)),
+            pl.BlockSpec((*x.shape[:2], width), lambda i: (0, 0, i + skip)),
         ],
         out_specs=pl.BlockSpec((ROWS, width), lambda i: (0, i)),
         compiler_params=PARAMS,
@@ -167,11 +178,39 @@
     return jnp.where(lane < HALF - k * NF, near, far)
 
 
-def rest_kernel(w_ref, x_ref, p_ref, g_ref, _, s_ref, t_ref, part_ref, row_ref, sem):
+def middle_kernel(w_ref, x_ref, p_ref, g_ref, _, s_ref, out_ref, part_ref):
+    parts = (p_ref[...] + dot(w_ref[...], rows_of(x_ref))).astype(BF16)
+    emit(parts, s_ref)
+    emit(parts, part_ref)
+    out_ref[...] = g_ref[...] + gram_of(parts)
+
+
+def middle(w, x, p, g, s):
+    times = w.shape[1]
+    width = x.shape[2]
+    here = pl.BlockSpec(memory_space=pltpu.VMEM)
+    return pl.pallas_call(
+        middle_kernel,
+        grid=(1,),
+        out_shape=(
+            jax.ShapeDtypeStruct(s.shape, BF16),
+            jax.ShapeDtypeStruct((ROWS, HALF), F32),
+            jax.ShapeDtypeStruct((ROWS, width), BF16),
+        ),
+        in_specs=[here, here, here, here, pl.BlockSpec(memory_space=pl.ANY)],
+        out_specs=(pl.BlockSpec((ROWS, width), lambda i: (0, 0)), here, here),
+        input_output_aliases={4: 0},
+        compiler_params=SMALL,
+        cost_estimate=pl.CostEstimate(flops=2 * ROWS * times * width, bytes_accessed=2**22, transcendentals=0),
+        name="middle",
+    )(w, x, p, g, s)
+
+
+def rest_kernel(low, w_ref, x_ref, p_ref, g_ref, _, s_ref, t_ref, part_ref, row_ref, sem):
     width = x_ref.shape[2]
     parts = (p_ref[...] + dot(w_ref[...], rows_of(x_ref))).astype(BF16)
     emit(parts, part_ref)
-    save = pltpu.make_async_copy(part_ref, s_ref.at[:, pl.ds(0, width)], sem)
+    save = pltpu.make_async_copy(part_ref, s_ref.at[:, pl.ds(low, width)], sem)
     save.start()
     kept = jnp.where(same_freq(ROWS), g_ref[...] + gram_of(parts), 0.0)
     tables = kept.reshape(2 * NB, NF, HALF).sum(axis=1)
@@ -191,17 +230,21 @@
     save.wait()
 
 
-def rest(w, x, p, g, s, copies):
+def rest(w, x, p, g, s, low, copies):
     times = w.shape[1]
     width = x.shape[2]
     here = pl.BlockSpec(memory_space=pltpu.VMEM)
     there = pl.BlockSpec(memory_space=pl.ANY)
     return pl.pallas_call(
-        rest_kernel,
-        out_shape=(jax.ShapeDtypeStruct(s.shape, BF16), jax.ShapeDtypeStruct((copies, 8, 256), F32)),
+        functools.partial(rest_kernel, low),
+        out_shape=(
+            jax.ShapeDtypeStruct(s.shape, BF16),
+            jax.ShapeDtypeStruct((copies, 8, 256), F32),
+            jax.ShapeDtypeStruct((ROWS, width), BF16),
+        ),
         in_specs=[here, here, here, here, there],
-        out_specs=(there, here),
-        scratch_shapes=[pltpu.VMEM((ROWS, width), BF16), pltpu.VMEM((16, 256), F32), pltpu.SemaphoreType.DMA],
+        out_specs=(there, here, here),
+        scratch_shapes=[pltpu.VMEM((16, 256), F32), pltpu.SemaphoreType.DMA],
         input_output_aliases={4: 0},
         compiler_params=pltpu.CompilerParams(vmem_limit_bytes=16 * 2**20),
         cost_estimate=pl.CostEstimate(flops=2 * ROWS * times * width, bytes_accessed=2**22, transcendentals=0),
@@ -215,12 +258,8 @@
     return (col == row // NF * 2 * NF + part * NF + row % NF).astype(BF16)
 
 
-def power_kernel(denominator, t_ref, s_ref, o_ref, m_ref, in_ref, out_ref, in_sem, out_sem):
-    steps, _, width = in_ref.shape
-    loads = []
-    for i in range(steps):
-        loads.append(pltpu.make_async_copy(s_ref.at[:, pl.ds(i * width, width)], in_ref.at[i], in_sem.at[i]))
-        loads[i].start()
+def power_kernel(denominator, t_ref, *refs):
+    part_refs, (o_ref, m_ref, out_ref, sem) = refs[:-4], refs[-4:]
     sums = jnp.sum(t_ref[...], axis=0) / denominator
     real_rows = [sums[k : k + 1, :] for k in range(PAIRS + 1)]
     imag_rows = [jnp.zeros_like(real_rows[0])] + [sums[PAIRS + k : PAIRS + k + 1, :] for k in range(1, PAIRS + 1)]
@@ -243,33 +282,35 @@
             row = jnp.broadcast_to(table[b : b + 1], (NF, ROWS))
             m_ref[at : at + NF, :] = jnp.where(same, row, 0.0).astype(BF16)
     stores = []
-    for i in range(steps):
-        loads[i].wait()
-        out_ref[i] = dot(m_ref[...], in_ref[i])
-        stores.append(pltpu.make_async_copy(out_ref.at[i], o_ref.at[:, pl.ds(i * width, width)], out_sem.at[i]))
-        stores[i].start()
+    low = 0
+    for part_ref in part_refs:
+        for at in range(0, part_ref.shape[1], 512):
+            values = part_ref[:, at : at + 512]
+            cols = pl.ds(low, values.shape[1])
+            out_ref[:, low : low + values.shape[1]] = dot(m_ref[...], values)
+            stores.append(pltpu.make_async_copy(out_ref.at[:, cols], o_ref.at[:, cols], sem.at[len(stores)]))
+            stores[-1].start()
+            low += values.shape[1]
     for store in stores:
         store.wait()
 
 
-def power(t, s, denominator):
-    pts = s.shape[1]
-    steps = pts // WIDTH
+def power(t, parts, denominator):
+    pts = sum(part.shape[1] for part in parts)
+    here = pl.BlockSpec(memory_space=pltpu.VMEM)
     return pl.pallas_call(
         functools.partial(power_kernel, denominator),
         out_shape=jax.ShapeDtypeStruct((ROWS, pts), F32),
-        in_specs=[pl.BlockSpec(memory_space=pltpu.VMEM), pl.BlockSpec(memory_space=pl.ANY)],
+        in_specs=[here] * (1 + len(parts)),
         out_specs=pl.BlockSpec(memory_space=pl.ANY),
         scratch_shapes=[
             pltpu.VMEM((ROWS, ROWS), BF16),
-            pltpu.VMEM((steps, ROWS, WIDTH), BF16),
-            pltpu.VMEM((steps, ROWS, WIDTH), F32),
-            pltpu.SemaphoreType.DMA((steps,)),
-            pltpu.SemaphoreType.DMA((steps,)),
+            pltpu.VMEM((ROWS, pts), F32),
+            pltpu.SemaphoreType.DMA((8,)),
         ],
-        compiler_params=pltpu.CompilerParams(vmem_limit_bytes=65_300_000),
+        compiler_params=pltpu.CompilerParams(vmem_limit_bytes=16 * 2**20),
         name="power",
-    )(t, s)
+    )(t, *parts)
 
 
 def to_all(t, axes):
@@ -290,11 +331,13 @@
     x = snapshots.reshape(local, own * count)
 
     later = own - FIRST
+    low = later - LAST
     (first,) = pack(x, own, [(1, later, FIRST)])
     first = lax.ppermute(first, "zh", swap)
     (pass_on,) = pack(x, own, [(1, 0, later)])
     pass_on = exchange(pass_on, PLANE)
-    passed = lax.ppermute(pass_on, "zh", swap)
+    passed = lax.ppermute(pass_on[:, :, :low], "zh", swap)
+    last = lax.ppermute(pass_on[:, :, low:], "zh", swap)
     (mine,) = pack(x, own, [(0, 0, own)])
     x0 = exchange(mine, PLANE)
     side = lax.axis_index("zh")
@@ -304,12 +347,14 @@
     w1 = weights(block_starts, kept_freqs, times + (1 - side) * 128)
     first, w0, w1 = lax.optimization_barrier((first, w0, w1))
     first = exchange(first, PLANE)
-    p = partial(w0, x0, later, 640)
-    s, g = whole(w0, w1, x0, first, 256)
-    s, t = rest(w1, passed, p, g, s, lax.axis_size(("y", "x")))
+    p0 = partial(w0, x0, 0, low, 256)
+    p1 = partial(w0, x0, low, LAST, 256)
+    s, g, part2 = whole(w0, w1, x0, first, 256)
+    s, g, part0 = middle(w1, passed, p0, g, s)
+    s, t, part1 = rest(w1, last, p1, g, s, low, lax.axis_size(("y", "x")))
     t = exchange(t, ("y", "x")).sum(axis=0)
     t = to_all(t, ("zh", "zl", "c"))
-    out = power(t, s, float(NB * total))
+    out = power(t, (part0, part1, part2), float(NB * total))
     shape = (1, NB, 2, NF, own)
     return s.reshape(shape), out.reshape(shape)
 

time: 178 us -> 189 us (1.062)
  starting transfers between devices: 30.9 us -> 47.2 us
  blocking collectives: 60.1 us -> 53.7 us
  local copies, waits for them, and re-layouts: 2.84 us -> 4.84 us
    all_to_all x3, waiting for transfers between devices: 27.2 us -> 16.1 us  [exchange(): return lax.all_to_all(x, axes, 0, 0, tiled=True)]
    all_to_all x3, starting transfers between devices: 23.8 us -> 34.1 us  [exchange(): return lax.all_to_all(x, axes, 0, 0, tiled=True)]
    ppermute x1 -> x2, waiting for transfers between devices: 9.86 us -> 18.7 us  [the longest x1 11.7 us: shards(): last = lax.ppermute(pass_on[:, :, low:], 'zh', swap)]
    all_to_all x1, blocking collectives: 46.7 us -> 40.5 us  [to_all(): return lax.all_to_all(copies, axes, 0, 0, tiled=True)]
    ppermute x1 -> x2, starting transfers between devices: 0.12 us -> 6.13 us  [the longest x1 6.13 us: shards(): passed = lax.ppermute(pass_on[:, :, :low], 'zh', swap)]
    slice x0 -> x2, local copies, waits for them, and re-layouts: none -> 3.94 us  [the longest x1 2.07 us: shards(): passed = lax.ppermute(pass_on[:, :, :low], 'zh', swap)]
    pallas_call x1 -> x2, Pallas kernels: 3.31 us -> 6.25 us  [partial(): pl.pallas_call(partial_kernel, grid=(pts // width,), out_shape=jax.ShapeD...]
    unnamed x16 -> x18, local copies, waits for them, and re-layouts: 2.82 us -> 0.88 us
  transfers between devices with their start and end apart: 5 -> 6, of which waited for: 4 -> 4; matrix products, arithmetic and copies ran while one was open for 3% -> 5% of each run, Pallas kernels for 8% -> 10%
where the time goes in v4:
time: 189 us; the launch traced here: 188 us
  blocking collectives  53.7 us (28%)
  waiting for transfers between devices  50.9 us (27%)
  starting transfers between devices  47.2 us (25%)
  Pallas kernels  25.8 us (14%)
  other arithmetic  5.13 us (3%)
  local copies, waits for them, and re-layouts  4.84 us (3%)
    all_to_all x1, blocking collectives, to_all(): return lax.all_to_all(copies, axes, 0, 0, tiled=True)  40.5 us
    all_to_all x3, starting transfers between devices, exchange(): return lax.all_to_all(x, axes, 0, 0, tiled=True)  34.1 us
    all_to_all x3, waiting for transfers between devices, exchange(): return lax.all_to_all(x, axes, 0, 0, tiled=True)  16.1 us
    ppermute x1, waiting for transfers between devices, shards(): first = lax.ppermute(first, 'zh', swap)  16.1 us
    all_to_all x1, blocking collectives, exchange(): return lax.all_to_all(x, axes, 0, 0, tiled=True)  13.2 us
    ppermute x1, waiting for transfers between devices, shards(): last = lax.ppermute(pass_on[:, :, low:], 'zh', swap)  11.7 us
    pallas_call x3, Pallas kernels, pack(): pl.pallas_call(functools.partial(pack_kernel, own, [job[:2] for job in jo...  8.1 us
    ppermute x1, starting transfers between devices, shards(): first = lax.ppermute(first, 'zh', swap)  7 us
  transfers between devices with their start and end apart: 6, of which 4 were waited for; matrix products, arithmetic and copies ran while one was open for 5% of the time, Pallas kernels for 10%

profile of v4, /device:TPU:1, one launch (start us, length us, event | category | flops | bytes accessed | tf_op | source)
XLA Modules:
  0.0 188.3 jit_solution(15575571795038579499)
XLA Ops:
  0.6 2.6 %pack.4 = bf16[32,16,1280]{2,1,0:T(8,128)(2,1)} custom-call(bf16[16,131072]{1,0:T(8,128)(2,1)} %bitcast.11), custom_call_target="tpu_custom_call" | custom-call | tf_op jit(solution)/shard_map/pack/pallas_call | solution.py:76
  3.3 8.6 %all-to-all-start = ((bf16[32,16,1280]{2,1,0:T(8,128)(2,1)}), bf16[32,16,1280]{2,1,0:T(8,128)(2,1)}, u32[]{:S(2)}, u32[]{:S(2)}) async-start(bf16[32,16,1280]{2,1,0:T(8,128)(2,1)} %pack.4), calls=%async_computation | async-start | bytes 2621440 | tf_op jit(solution)/shard_map/all_to_all | solution.py:322
  11.9 3.2 %pack.5 = bf16[32,16,2048]{2,1,0:T(8,128)(2,1)} custom-call(bf16[16,131072]{1,0:T(8,128)(2,1)} %bitcast.12), custom_call_target="tpu_custom_call" | custom-call | tf_op jit(solution)/shard_map/pack/pallas_call | solution.py:76
  15.1 16.1 %all-to-all-done = bf16[32,16,1280]{2,1,0:T(8,128)(2,1)} async-done(((bf16[32,16,1280]{2,1,0:T(8,128)(2,1)}), bf16[32,16,1280]{2,1,0:T(8,128)(2,1)}, u32[]{:S(2)}, u32[]{:S(2)}) %all-to-all-start) | async-done | bytes 1310752 | tf_op jit(solution)/shard_map/all_to_all | solution.py:322
  31.3 5.2 %all-to-all-start.1 = ((bf16[32,16,2048]{2,1,0:T(8,128)(2,1)}), bf16[32,16,2048]{2,1,0:T(8,128)(2,1)S(1)}, u32[]{:S(2)}, u32[]{:S(2)}) async-start(bf16[32,16,2048]{2,1,0:T(8,128)(2,1)} %pack.5), calls=%async_computation.1 | async-start | bytes 4194304 | tf_op jit(solution)/shard_map/all_to_all | solution.py:322
  36.4 0.0 copy-start.7
  36.4 0.0 copy-start.8
  36.5 2.3 %pack.3 = bf16[32,16,768]{2,1,0:T(8,128)(2,1)} custom-call(bf16[16,131072]{1,0:T(8,128)(2,1)} %bitcast.13), custom_call_target="tpu_custom_call" | custom-call | tf_op jit(solution)/shard_map/pack/pallas_call | solution.py:76
  38.7 7.0 %collective-permute-start = (bf16[32,16,768]{2,1,0:T(8,128)(2,1)}, bf16[32,16,768]{2,1,0:T(8,128)(2,1)}, u32[]{:S(2)}, u32[]{:S(2)}) collective-permute-start(bf16[32,16,768]{2,1,0:T(8,128)(2,1)} %pack.3), channel_id=1, source_target_pairs={{0,32},{32,0},{1,33},{33,1},{2,34},{34,2},{3,35},{35,3},{4,36},{36... | collective-permute-start | bytes 2359304 | tf_op jit(solution)/shard_map/ppermute | solution.py:336
  45.7 0.1 subtract_select_fusion
  45.8 0.2 fusion.15
  46.0 4.0 %multiply_convert_fusion.1 = (bf16[1,7,32,512]{3,2,1,0:T(8,128)(2,1)S(1)}, bf16[1,7,32,512]{3,2,1,0:T(8,128)(2,1)S(1)}, bf16[1,7,32,512]{3,2,1,0:T(8,128)(2,1)S(1)}, bf16[1,7,32,512]{3,2,1,0:T(8,128)(2,1)S(1)}) fusion(f32[7,512]{1,0:T(8,128)S(1)} %get-tuple-element.30, s32[7,512]{1,0:T(8,128)S(1)} %get-tuple-element.38, s32[32]{0:T(128)S(1)} %copy-done.8, ...), kind=kLoop, calls=%fused_computation.19 | loop fusion | flops 4587520 | bytes 1003648 | tf_op jit(solution)/shard_map/convert
  50.0 0.8 pad_maximum_fusion
  50.9 16.1 %collective-permute-done = bf16[32,16,768]{2,1,0:T(8,128)(2,1)} collective-permute-done((bf16[32,16,768]{2,1,0:T(8,128)(2,1)}, bf16[32,16,768]{2,1,0:T(8,128)(2,1)}, u32[]{:S(2)}, u32[]{:S(2)}) %collective-permute-start) | collective-permute-done | bytes 786464 | tf_op jit(solution)/shard_map/ppermute | solution.py:336
  67.0 0.0 all-to-all-done.1.x_ref.x0_ref
  67.0 20.3 %all-to-all-start.2 = ((bf16[32,16,768]{2,1,0:T(8,128)(2,1)}), bf16[32,16,768]{2,1,0:T(8,128)(2,1)}, u32[]{:S(2)}, u32[]{:S(2)}) async-start(bf16[32,16,768]{2,1,0:T(8,128)(2,1)} %collective-permute-done), calls=%async_computation.2 | async-start | bytes 1572864 | tf_op jit(solution)/shard_map/all_to_all | solution.py:322
  87.2 2.1 %slice.9 = bf16[32,16,768]{2,1,0:T(8,128)(2,1)} slice(bf16[32,16,1280]{2,1,0:T(8,128)(2,1)} %all-to-all-done), slice={[0:32], [0:16], [0:768]} | slice | bytes 1572864 | tf_op jit(solution)/shard_map/slice | solution.py:339
  89.3 6.1 %collective-permute-start.2 = (bf16[32,16,768]{2,1,0:T(8,128)(2,1)}, bf16[32,16,768]{2,1,0:T(8,128)(2,1)}, u32[]{:S(2)}, u32[]{:S(2)}) collective-permute-start(bf16[32,16,768]{2,1,0:T(8,128)(2,1)} %slice.9), channel_id=1, source_target_pairs={{0,32},{32,0},{1,33},{33,1},{2,34},{34,2},{3,35},{35,3},{4,36},{36... | collective-permute-start | bytes 2359304 | tf_op jit(solution)/shard_map/ppermute | solution.py:339
  95.4 1.9 slice.8
  97.3 0.0 collective-permute-start.1
  97.3 2.5 %partial.2.p_ref = f32[448,512]{1,0:T(8,128)} custom-call(bf16[448,512]{1,0:T(8,128)(2,1)} %bitcast.8, bf16[32,16,2048]{2,1,0:T(8,128)(2,1)} %copy-done), custom_call_target="tpu_custom_call" | custom-call | flops 234881024 | bytes 2097152 | tf_op jit(solution)/shard_map/partial/pallas_call | solution.py:155
  99.8 3.7 %partial.3.p_ref = f32[448,768]{1,0:T(8,128)} custom-call(bf16[448,512]{1,0:T(8,128)(2,1)} %bitcast.9, bf16[32,16,2048]{2,1,0:T(8,128)(2,1)} %copy-done), custom_call_target="tpu_custom_call" | custom-call | flops 352321536 | bytes 2097152 | tf_op jit(solution)/shard_map/partial/pallas_call | solution.py:155
  103.6 0.0 all-to-all-done.2.x1_ref
  103.6 4.5 %whole.1 = (bf16[448,2048]{1,0:T(8,128)(2,1)}, f32[448,224]{1,0:T(8,128)S(1)}, bf16[448,768]{1,0:T(8,128)(2,1)S(1)}) custom-call(bf16[448,512]{1,0:T(8,128)(2,1)S(1)} %bitcast.10, bf16[448,512]{1,0:T(8,128)(2,1)S(1)} %bitcast.5, bf16[32,16,2048]{2,1,0:T(8,128)(2,1)S(1)} %copy-done.1, bf16[32,16,768]{2,1,0:T(8,128)(2,1)} %all-to-all-done.2.x1_ref), custom_call_target="tpu_custom_call" | custom-call | flops 704643072 | bytes 4194304 | tf_op jit(solution)/shard_map/whole/pallas_call | solution.py:123
  108.1 0.8 copy-done.5
  109.0 7.0 %collective-permute-done.2.x_ref = bf16[32,16,768]{2,1,0:T(8,128)(2,1)} collective-permute-done((bf16[32,16,768]{2,1,0:T(8,128)(2,1)}, bf16[32,16,768]{2,1,0:T(8,128)(2,1)}, u32[]{:S(2)}, u32[]{:S(2)}) %collective-permute-start.2) | collective-permute-done | bytes 786464 | tf_op jit(solution)/shard_map/ppermute | solution.py:339
  115.9 2.7 %middle.1 = (bf16[448,2048]{1,0:T(8,128)(2,1)}, f32[448,224]{1,0:T(8,128)S(1)}, bf16[448,768]{1,0:T(8,128)(2,1)S(1)}) custom-call(bf16[448,512]{1,0:T(8,128)(2,1)S(1)} %bitcast.6, bf16[32,16,768]{2,1,0:T(8,128)(2,1)} %collective-permute-done.2.x_ref, f32[448,768]{1,0:T(8,128)S(1)} %copy-done.3, ...), custom_call_target="tpu_custom_call", output_to_operand_aliasing={{0}: (4, {})} | custom-call | flops 352321536 | bytes 4194304 | tf_op jit(solution)/shard_map/middle/pallas_call | solution.py:192
  118.6 11.7 %collective-permute-done.1.x_ref = bf16[32,16,512]{2,1,0:T(8,128)(2,1)S(1)} collective-permute-done((bf16[32,16,512]{2,1,0:T(8,128)(2,1)}, bf16[32,16,512]{2,1,0:T(8,128)(2,1)S(1)}, u32[]{:S(2)}, u32[]{:S(2)}) %collective-permute-start.1) | collective-permute-done | bytes 524320 | tf_op jit(solution)/shard_map/ppermute | solution.py:340
  130.3 1.4 rest.1
  131.8 13.2 %all_to_all.25 = f32[16,8,256]{2,1,0:T(8,128)S(1)} all-to-all(f32[16,8,256]{2,1,0:T(8,128)S(1)} %get-tuple-element.22), channel_id=1, replica_groups=mesh['y'=4,'zh'=2,'x'=4,'c'=2,'zl'=4] {'y','x'}, dimensions={0} | all-to-all | bytes 262144 | tf_op jit(solution)/shard_map/all_to_all | solution.py:322
  145.0 40.5 %all_to_all.26.t_ref = f32[16,8,256]{2,1,0:T(8,128)S(1)} all-to-all(f32[16,8,256]{2,1,0:T(8,128)S(1)} %broadcast_in_dim.11), channel_id=1, replica_groups=mesh['y'=4,'zh'=2,'x'=4,'c'=2,'zl'=4] {'zh','zl','c'}, dimensions={0} | all-to-all | bytes 262144 | tf_op jit(solution)/shard_map/all_to_all | solution.py:318
  185.5 2.8 %power.1 = f32[448,2048]{1,0:T(8,128)} custom-call(f32[16,8,256]{2,1,0:T(8,128)S(1)} %all_to_all.26.t_ref, bf16[448,768]{1,0:T(8,128)(2,1)S(1)} %get-tuple-element.23.refs_0_, bf16[448,512]{1,0:T(8,128)(2,1)S(1)} %get-tuple-element.24.refs_1_, bf16[448,768]{1,0:T(8,128)(2,1)S(1)} %copy-done.6), custom_call_target="tpu_custom_call" | custom-call | tf_op jit(solution)/shard_map/power/pallas_call | solution.py:301
  (19 shorter events, 0.1 us)
Async XLA Ops:
  3.3 28.0 %all-to-all-start = ((bf16[32,16,1280]{2,1,0:T(8,128)(2,1)}), bf16[32,16,1280]{2,1,0:T(8,128)(2,1)}, u32[]{:S(2)}, u32[]{:S(2)}) async-start(bf16[32,16,1280]{2,1,0:T(8,128)(2,1)} %pack.4), calls=%async_computation | async-start | bytes 2621440 | tf_op jit(solution)/shard_map/all_to_all | solution.py:322
  31.3 35.7 %all-to-all-start.1 = ((bf16[32,16,2048]{2,1,0:T(8,128)(2,1)}), bf16[32,16,2048]{2,1,0:T(8,128)(2,1)S(1)}, u32[]{:S(2)}, u32[]{:S(2)}) async-start(bf16[32,16,2048]{2,1,0:T(8,128)(2,1)} %pack.5), calls=%async_computation.1 | async-start | bytes 4194304 | tf_op jit(solution)/shard_map/all_to_all | solution.py:322
  36.4 9.3 %copy-start.7 = (s32[7]{0:T(128)S(1)}, s32[7]{0:T(128)}, u32[]{:S(2)}) copy-start(s32[7]{0:T(128)} %param.4) | copy-start | bytes 88
  36.4 9.6 %copy-start.8 = (s32[32]{0:T(128)S(1)}, s32[32]{0:T(128)}, u32[]{:S(2)}) copy-start(s32[32]{0:T(128)} %param.5) | copy-start | bytes 388
  38.7 28.2 %collective-permute-start = (bf16[32,16,768]{2,1,0:T(8,128)(2,1)}, bf16[32,16,768]{2,1,0:T(8,128)(2,1)}, u32[]{:S(2)}, u32[]{:S(2)}) collective-permute-start(bf16[32,16,768]{2,1,0:T(8,128)(2,1)} %pack.3), channel_id=1, source_target_pairs={{0,32},{32,0},{1,33},{33,1},{2,34},{34,2},{3,35},{35,3},{4,36},{36... | collective-permute-start | bytes 2359304 | tf_op jit(solution)/shard_map/ppermute | solution.py:336
  67.0 30.4 %copy-start = (bf16[32,16,2048]{2,1,0:T(8,128)(2,1)}, bf16[32,16,2048]{2,1,0:T(8,128)(2,1)S(1)}, u32[]{:S(2)}) copy-start(bf16[32,16,2048]{2,1,0:T(8,128)(2,1)S(1)} %all-to-all-done.1.x_ref.x0_ref) | copy-start | bytes 6291460
  67.0 36.6 %all-to-all-start.2 = ((bf16[32,16,768]{2,1,0:T(8,128)(2,1)}), bf16[32,16,768]{2,1,0:T(8,128)(2,1)}, u32[]{:S(2)}, u32[]{:S(2)}) async-start(bf16[32,16,768]{2,1,0:T(8,128)(2,1)} %collective-permute-done), calls=%async_computation.2 | async-start | bytes 1572864 | tf_op jit(solution)/shard_map/all_to_all | solution.py:322
  89.3 26.6 %collective-permute-start.2 = (bf16[32,16,768]{2,1,0:T(8,128)(2,1)}, bf16[32,16,768]{2,1,0:T(8,128)(2,1)}, u32[]{:S(2)}, u32[]{:S(2)}) collective-permute-start(bf16[32,16,768]{2,1,0:T(8,128)(2,1)} %slice.9), channel_id=1, source_target_pairs={{0,32},{32,0},{1,33},{33,1},{2,34},{34,2},{3,35},{35,3},{4,36},{36... | collective-permute-start | bytes 2359304 | tf_op jit(solution)/shard_map/ppermute | solution.py:339
  97.3 33.0 %collective-permute-start.1 = (bf16[32,16,512]{2,1,0:T(8,128)(2,1)}, bf16[32,16,512]{2,1,0:T(8,128)(2,1)S(1)}, u32[]{:S(2)}, u32[]{:S(2)}) collective-permute-start(bf16[32,16,512]{2,1,0:T(8,128)(2,1)} %slice.8), channel_id=1, source_target_pairs={{0,32},{32,0},{1,33},{33,1},{2,34},{34,2},{3,35},{35,3},{4,36},{36... | collective-permute-start | bytes 1572872 | tf_op jit(solution)/shard_map/ppermute | solution.py:340
  99.8 3.7 %copy-start.1 = (bf16[32,16,2048]{2,1,0:T(8,128)(2,1)S(1)}, bf16[32,16,2048]{2,1,0:T(8,128)(2,1)}, u32[]{:S(2)}) copy-start(bf16[32,16,2048]{2,1,0:T(8,128)(2,1)} %copy-done) | copy-start | bytes 6291460
  99.8 3.7 %copy-start.2 = (bf16[2,7,32,512]{3,2,1,0:T(8,128)(2,1)S(1)}, bf16[2,7,32,512]{3,2,1,0:T(8,128)(2,1)}, u32[]{:S(2)}) copy-start(bf16[2,7,32,512]{3,2,1,0:T(8,128)(2,1)} %pad_maximum_fusion) | copy-start | bytes 1376260
  103.6 12.3 %copy-start.3 = (f32[448,768]{1,0:T(8,128)S(1)}, f32[448,768]{1,0:T(8,128)}, u32[]{:S(2)}) copy-start(f32[448,768]{1,0:T(8,128)} %partial.3.p_ref) | copy-start | bytes 4128772
  108.1 0.8 copy-start.5
  115.9 14.4 %copy-start.4 = (f32[448,512]{1,0:T(8,128)S(1)}, f32[448,512]{1,0:T(8,128)}, u32[]{:S(2)}) copy-start(f32[448,512]{1,0:T(8,128)} %partial.2.p_ref) | copy-start | bytes 2752516
  130.3 55.1 %copy-start.6 = (bf16[448,768]{1,0:T(8,128)(2,1)S(1)}, bf16[448,768]{1,0:T(8,128)(2,1)}, u32[]{:S(2)}) copy-start(bf16[448,768]{1,0:T(8,128)(2,1)} %copy-done.5) | copy-start | bytes 2064388
